TPU v7x, 32 devices: a whole 2x2x4 slice. The times are simulated.
32 devices in a mesh: slab: 4 (over y, x), sub: 8 (over z, core).
Axes of the slice: x: 2, y: 2, z: 4, core: 2. Of those that a mesh axis runs over, the one named last changes fastest.
Arguments:
- offsets: float32 [3, 4, 8, 64, 128], P(None, None, 'slab', 'sub'), may hold values from -0.5 to 0.5
- velocities: float32 [3, 4, 8, 64, 128], P(None, None, 'slab', 'sub'), may hold values from -6 to 6
- chain_label: int32 [4, 8, 64, 128], P(None, 'slab', 'sub'), may hold values from -1 to 31999, as said below
- partners: int32 [2, 4, 8, 64, 128], P(None, None, 'slab', 'sub'), may hold values from 16 to 91, as said below
- anchored: int32 [4, 8, 64, 128], P(None, 'slab', 'sub'), may hold values 0 or 1
Outputs:
- positions: float32 [3, 4, 8, 64, 128], P(None, None, 'slab', 'sub')
- half_velocity: float32 [3, 4, 8, 64, 128], P(None, None, 'slab', 'sub')
- unit_force: float32 [3, 4, 8, 64, 128], P(None, None, 'slab', 'sub')
Inputs may be any that keep to these rules, and one draw needn't show every extreme that they name: `chain_label`: beads that carry equal labels within one cell's neighbourhood belong to one loop; -1 marks an empty slot. `partners`: the two codes of a bead name the previous and the next bead of its own loop, in a neighbouring cell, and that bead names it back; every loop is closed. The codes of an empty slot are its own code.
All inputs are finite; a program needn't handle non-finite values. No bound on the sum of `anchored` on one device may be relied on, other than what follows from the above.
Results may differ from a plain program's by a relative error of at most 0.0003.
Values sent between devices are 32-bit elements; how exact they have to be, the bound alone decides.
No kernel may reach another device: no remote copies, remote signals or barrier semaphores. Data moves between devices by JAX's collectives and lax.ppermute only.
A program may use at most 64 MiB of HBM per device.

v0:
```python
import jax
import jax.numpy as jnp
from jax import lax
from jax.experimental import pallas as pl
from jax.experimental.pallas import tpu as pltpu
from jax.sharding import PartitionSpec as P

DESCENTS = 3

cell_width = 1.25
soft_floor = 0.64
bond_stiff = 100.0
fene_floor = 0.2
time_step = 0.01
half_step = 0.005
half_step_sq = 5e-05
step_length = 0.1
tiny_eps = 1e-06

force_scale = 48.0
bond_range_sq = 9.0
live_barrier = 0.5
dead_barrier = 4.0
bond_unit = -bond_stiff * bond_range_sq / force_scale
code_low, code_high = 16, 91

vmem_limit = 12 << 20


def row_select(tile, row, index):
    rows = lax.broadcasted_iota(jnp.int32, tile.shape, 0)
    return jnp.where(rows == index, jnp.broadcast_to(row, tile.shape), tile)


def spread(main, low, high, shift_y, shift_z, store):
    rows, lanes = main.shape
    for step_y in (-1, 0, 1):
        tile = main
        if step_y == -1:
            tile = row_select(pltpu.roll(main, 1, 0), low, 0)
        elif step_y == 1:
            tile = row_select(pltpu.roll(main, rows - 1, 0), high, rows - 1)
        if shift_y and step_y:
            tile = tile + step_y * cell_width
        for step_z in (-1, 0, 1):
            moved = tile
            if step_z == -1:
                moved = pltpu.roll(tile, 1, 1)
            elif step_z == 1:
                moved = pltpu.roll(tile, lanes - 1, 1)
            if shift_z and step_z:
                moved = moved + step_z * cell_width
            store((step_y + 1) * 3 + step_z + 1, moved)


class Field:
    def __init__(self, refs, planes, channels, rows):
        self.own, self.low, self.high, self.down, self.up = refs
        self.planes, self.channels, self.rows = planes, channels, rows

    def plane(self, plane, channel):
        rows = self.rows
        if 1 <= plane <= self.planes:
            return (
                self.own[plane - 1, channel],
                self.low[plane - 1, pl.ds(channel, 1)],
                self.high[plane - 1, pl.ds(channel, 1)],
            )
        edge = self.down if plane == 0 else self.up
        base = self.channels * rows
        half = (edge.shape[0] - base) // 2
        return (
            edge[pl.ds(channel * rows, rows)],
            edge[pl.ds(base + channel, 1)],
            edge[pl.ds(base + half + channel, 1)],
        )


def pair_terms(own, other, barrier):
    sep = [a - b for a, b in zip(own, other)]
    dist_sq = sep[0] * sep[0] + sep[1] * sep[1] + sep[2] * sep[2]
    inv = 1.0 / jnp.maximum(dist_sq, soft_floor)
    inv_two = inv * inv
    coef = (inv_two * inv_two) * jnp.maximum(inv_two * inv - barrier, 0.0)
    return sep, dist_sq, coef


def bond_coef(dist_sq, strength):
    return strength * (1.0 / jnp.maximum(bond_range_sq - dist_sq, bond_range_sq * fene_floor))


def bond_cells(slots):
    return code_low // slots, code_high // slots + 1


def cell_runs(slots):
    bond_from, bond_to = bond_cells(slots)
    marks = sorted({0, 9, 18, 27, bond_from, bond_to})
    return [(a, b, a >= bond_from and b <= bond_to) for a, b in zip(marks, marks[1:])]


def sweep(slots, planes, own_tile, near, body):
    totals = []
    for plane in range(planes):
        own = [own_tile(plane, c) for c in range(3 * slots)]
        acc = [jnp.zeros_like(own[0]) for _ in range(3 * slots)]
        for first, last, bonded in cell_runs(slots):
            step_x = first // 9 - 1
            moved = [own[s] - step_x * cell_width for s in range(slots)] + own[slots:]

            def step(cell, acc, moved=moved, bonded=bonded, plane=plane):
                acc = list(acc)
                for s2 in range(slots):
                    other = [near[plane * 9 + cell, c * slots + s2] for c in range(3)]
                    each = body(plane, cell, s2, other, bonded)
                    for s1 in range(slots):
                        coef, sep = each(s1, [moved[c * slots + s1] for c in range(3)])
                        for c in range(3):
                            acc[c * slots + s1] = acc[c * slots + s1] + coef * sep[c]
                return tuple(acc)

            acc = lax.fori_loop(first, last, step, tuple(acc))
        totals.append(list(acc))
    return totals


def put_rows(low_ref, high_ref, plane, channel, tile):
    rows = tile.shape[0]
    low_ref[plane, pl.ds(channel, 1)] = tile[0:1]
    high_ref[plane, pl.ds(channel, 1)] = tile[rows - 1 : rows]


def prepare_kernel(wide_ref, field_ref, low_ref, high_ref):
    channels, planes, _, _ = wide_ref.shape
    for plane in range(planes):
        for c in range(channels):
            tile = wide_ref[c, plane]
            field_ref[plane, c] = tile
            put_rows(low_ref, high_ref, plane, c, tile)


def verlet_kernel(
    extra_ref, own, low, high, down, up,
    half_ref, next_ref, next_low, next_high, barrier_ref, weight_ref, near,
):
    _, slots, planes, rows, _ = half_ref.shape
    vel_at, partner_at, anchor_at = 0, 3 * slots, 5 * slots
    field = Field((own, low, high, down, up), planes, 4 * slots, rows)
    for plane in range(planes + 2):
        for c in range(4 * slots):

            def store(k, tile, plane=plane, c=c):
                near[plane * 9 + k, c] = tile

            main, lo, hi = field.plane(plane, c)
            spread(main, lo, hi, c // slots == 1, c // slots == 2, store)

    def body(plane, cell, s2, other, bonded):
        label = near[plane * 9 + cell, 3 * slots + s2]
        alive = jnp.where(label < 0.0, dead_barrier, live_barrier)

        def each(s1, mine):
            sep, dist_sq, coef = pair_terms(mine, other, alive)
            barrier = jnp.where(label == own[plane, 3 * slots + s1], dead_barrier, alive)
            if bonded:
                code = (cell * slots + s2).astype(jnp.float32)
                strength = jnp.where(extra_ref[partner_at + s1, plane] == code, bond_unit, 0.0)
                strength += jnp.where(extra_ref[partner_at + slots + s1, plane] == code, bond_unit, 0.0)
                barrier = jnp.where(strength < 0.0, dead_barrier - strength, barrier)
                coef += bond_coef(dist_sq, strength)
            pending.append(barrier)
            if len(pending) == 2:
                both = jnp.concatenate(pending, axis=0).astype(barrier_ref.dtype)
                barrier_ref[plane * 27 + cell, (s2 * slots + s1) // 2] = both
                pending.clear()
            return coef, sep

        return each

    pending = []
    totals = sweep(slots, planes, lambda plane, c: own[plane, c], near, body)
    for plane in range(planes):
        for s in range(slots):
            free = ((own[plane, 3 * slots + s] >= 0.0) & (extra_ref[anchor_at + s, plane] == 0.0)).astype(jnp.float32)
            weight_ref[plane, s] = free * force_scale
            for c in range(s, 3 * slots, slots):
                force = totals[plane][c] * (free * force_scale)
                moving = free * extra_ref[vel_at + c, plane]
                half_ref[c // slots, s, plane] = moving + half_step * force
                place = own[plane, c] + (time_step * moving + half_step_sq * force)
                next_ref[plane, c] = place
                put_rows(next_low, next_high, plane, c, place)


def inverse_peak(peaks):
    peak_force = jnp.sqrt(jnp.max(jnp.max(peaks, axis=0, keepdims=True), axis=1, keepdims=True))
    return 1.0 / (peak_force + tiny_eps)


def descent_kernel(slots, planes, rows, moves, last, *refs):
    refs = list(refs)

    def take(count):
        taken = refs[:count]
        del refs[:count]
        return taken

    ids, barrier_ref, weight_ref = take(3)
    places = take(5)
    if moves:
        own, low, high, down, up, mixed = take(6)
        now = take(1) + refs[-4:] if last else take(5)
        if last:
            del refs[-4:]
        scale = step_length * inverse_peak(mixed[:, mixed.shape[1] - 1, :])
        for i, by in enumerate((own, low, high)):
            now[i][...] = places[i][...] + scale.reshape((1,) * len(by.shape)) * by[...]
        for i, by, corners in ((3, down, (3, 2)), (4, up, (1, 0))):
            base, pad = by.shape[0], mixed.shape[1]
            now[i][pl.ds(0, base)] = places[i][pl.ds(0, base)] + scale * by[...]
            for side, corner in enumerate(corners):
                at = pl.ds(base + side * pad, pad)
                now[i][at] = places[i][at] + scale * mixed[ids[corner]]
        places = now
    field = Field(places, planes, 3 * slots, rows)
    if last:
        force_ref, peak_ref, near = refs
    else:
        force_ref, force_low, force_high, mix_ref, near = refs
    for plane in range(planes + 2):
        for c in range(3 * slots):

            def store(k, tile, plane=plane, c=c):
                near[plane * 9 + k, c] = tile

            main, lo, hi = field.plane(plane, c)
            spread(main, lo, hi, c // slots == 1, c // slots == 2, store)

    def body(plane, cell, s2, other, bonded):
        both = [
            barrier_ref[plane * 27 + cell, (s2 * slots) // 2 + i].astype(jnp.float32)
            for i in range(slots // 2)
        ]

        def each(s1, mine):
            barrier = both[s1 // 2][(s1 % 2) * rows : (s1 % 2 + 1) * rows]
            sep, dist_sq, coef = pair_terms(mine, other, barrier)
            if bonded:
                coef += bond_coef(dist_sq, jnp.minimum(dead_barrier - barrier, 0.0))
            return coef, sep

        return each

    totals = sweep(slots, planes, lambda plane, c: field.own[plane, c], near, body)
    peak = None
    for plane in range(planes):
        forces = [total * weight_ref[plane, c % slots] for c, total in enumerate(totals[plane])]
        for c in range(3 * slots):
            force_ref[plane, c] = forces[c]
            if not last:
                put_rows(force_low, force_high, plane, c, forces[c])
        for s in range(slots):
            size = sum(forces[c * slots + s] * forces[c * slots + s] for c in range(3))
            peak = size if peak is None else jnp.maximum(peak, size)
    peak = jnp.max(peak, axis=0, keepdims=True)
    if last:
        peak_ref[...] = jnp.broadcast_to(peak, peak_ref.shape)
        return

    def fill(device, carry):
        mix_ref[device] = jnp.broadcast_to(peak, mix_ref.shape[1:])
        return carry

    lax.fori_loop(0, mix_ref.shape[0], fill, 0)
    for corner in range(4):
        plane = planes - 1 if corner < 2 else 0
        rows_ref = force_high if corner % 2 == 0 else force_low
        mix_ref[ids[corner], pl.ds(0, 3 * slots)] = rows_ref[plane, pl.ds(0, 3 * slots)]


def finish_kernel(place_ref, force_ref, peaks_ref, pos_ref, unit_ref):
    slots, planes = pos_ref.shape[1], pos_ref.shape[2]
    inverse = inverse_peak(peaks_ref[...])
    scale = step_length * inverse
    for plane in range(planes):
        for c in range(3 * slots):
            force = force_ref[plane, c]
            unit_ref[c // slots, c % slots, plane] = inverse * force
            pos_ref[c // slots, c % slots, plane] = place_ref[plane, c] + scale * force


def ring(axis):
    count = lax.axis_size(axis)
    forward = [(i, (i + 1) % count) for i in range(count)]
    return forward, [(b, a) for a, b in forward]


def halo(own, first_rows, last_rows):
    planes, channels, rows, lanes = own.shape
    forward, backward = ring("sub")
    low = lax.ppermute(last_rows, "sub", forward)
    high = lax.ppermute(first_rows, "sub", backward)

    def packed(plane):
        return jnp.concatenate(
            [own[plane].reshape(channels * rows, lanes), low[plane], high[plane]], axis=0
        )

    forward, backward = ring("slab")
    down = lax.ppermute(packed(planes - 1), "slab", forward)
    up = lax.ppermute(packed(0), "slab", backward)
    return (own, low, high, down, up)


def near_halo(own, first_rows, last_rows):
    planes, channels, rows, lanes = own.shape
    forward, backward = ring("sub")
    low = lax.ppermute(last_rows, "sub", forward)
    high = lax.ppermute(first_rows, "sub", backward)
    forward, backward = ring("slab")
    flat = (channels * rows, lanes)
    down = lax.ppermute(own[planes - 1].reshape(flat), "slab", forward)
    up = lax.ppermute(own[0].reshape(flat), "slab", backward)
    return (own, low, high, down, up)


def corner_devices():
    slabs, subs = lax.axis_size("slab"), lax.axis_size("sub")
    x, y = lax.axis_index("slab"), lax.axis_index("sub")
    return jnp.stack(
        [
            ((x + i + slabs) % slabs) * subs + (y + j + subs) % subs
            for i in (1, -1)
            for j in (1, -1)
        ]
    ).astype(jnp.int32)


def call(kernel, outs, scratch=(), flops=0, scalars=0, inputs=0):
    specs = {}
    if scalars:
        specs["in_specs"] = [pl.BlockSpec(memory_space=pltpu.SMEM)] * scalars
        specs["in_specs"] += [pl.BlockSpec(memory_space=pltpu.VMEM)] * (inputs - scalars)
    return pl.pallas_call(
        kernel,
        out_shape=[
            jax.ShapeDtypeStruct(shape, jnp.float32) if isinstance(shape, tuple) else shape
            for shape in outs
        ],
        scratch_shapes=[pltpu.VMEM(shape, jnp.float32) for shape in scratch],
        compiler_params=pltpu.CompilerParams(vmem_limit_bytes=vmem_limit),
        cost_estimate=pl.CostEstimate(flops=flops, bytes_accessed=4 << 20, transcendentals=0),
        **specs,
    )


def shards(offsets, velocities, chain_label, partners, anchored):
    _, slots, planes, rows, lanes = offsets.shape
    devices = lax.axis_size("slab") * lax.axis_size("sub")
    padded = 4 * slots
    flops = planes * 27 * slots * slots * rows * lanes * 30
    tiles = (rows, lanes)
    field = (planes, 3 * slots, *tiles)
    edge = (planes, padded, lanes)
    near = ((planes + 2) * 9, 3 * slots, *tiles)
    pairs = [
        jax.ShapeDtypeStruct(
            (planes * 27, slots * slots // 2, 2 * rows, lanes), jnp.bfloat16
        ),
        (planes, slots, *tiles),
    ]
    ids = corner_devices()
    flat = offsets.reshape(3 * slots, planes, *tiles)
    labels = chain_label.astype(jnp.float32)
    wide = jnp.concatenate([flat, labels], axis=0)
    start = halo(*call(prepare_kernel, [(planes, 4 * slots, *tiles), edge, edge])(wide))
    extra = jnp.concatenate(
        [
            velocities.reshape(3 * slots, planes, *tiles),
            partners.reshape(2 * slots, planes, *tiles).astype(jnp.float32),
            anchored.astype(jnp.float32),
        ],
        axis=0,
    )
    half_velocity, place, first, last, *pairs = call(
        verlet_kernel,
        [velocities.shape, field, edge, edge, *pairs],
        [((planes + 2) * 9, 4 * slots, *tiles)],
        flops,
    )(extra, *start)
    places = halo(place, first, last)
    moves = ()
    for descent in range(DESCENTS):
        final = descent + 1 == DESCENTS

        def kernel(*refs, moving=bool(moves), final=final):
            descent_kernel(slots, planes, rows, moving, final, *refs)

        outs = [field, (devices, lanes)] if final else [field, edge, edge, (devices, padded, lanes)]
        moved = [x.shape for x in places] if moves else []
        scratch = [near]
        if final:
            moved, scratch = moved[:1], scratch + moved[1:]
        operands = (ids, *pairs, *places, *moves)
        results = call(kernel, moved + outs, scratch, flops, 1, len(operands))(*operands)
        peaks = lax.all_to_all(results[-1], ("slab", "sub"), 0, 0, tiled=True)
        if final:
            place, force, _ = results
            break
        if moves:
            places, results = results[:5], results[5:]
        moves = (*near_halo(*results[:3]), peaks)
    positions, unit_force = call(finish_kernel, [offsets.shape, offsets.shape])(
        place, force, peaks
    )
    return (positions, half_velocity, unit_force)


def solution(mesh):
    return jax.shard_map(
        shards,
        mesh=mesh,
        in_specs=(
            P(None, None, "slab", "sub", None),
            P(None, None, "slab", "sub", None),
            P(None, "slab", "sub", None),
            P(None, None, "slab", "sub", None),
            P(None, "slab", "sub", None),
        ),
        out_specs=(
            P(None, None, "slab", "sub", None),
            P(None, None, "slab", "sub", None),
            P(None, None, "slab", "sub", None),
        ),
        check_vma=False,
    )
```

profile of v0, /device:TPU:0, one launch (start us, length us, event | category | flops | bytes accessed | tf_op | source)
XLA Modules:
  0.0 88.4 jit_solution(13396529857307820568)
XLA Ops:
  0.6 0.8 convert_element_type.15
  1.4 0.9 %pad_maximum_fusion.1.wide_ref = f32[16,2,8,128]{3,2,1,0:T(8,128)S(1)} fusion(f32[4,2,8,128]{3,2,1,0:T(8,128)S(1)} %convert_element_type.15, f32[12,2,8,128]{3,2,1,0:T(8,128)} %bitcast.46), kind=kLoop, calls=%fused_computation.1 | loop fusion | flops 32768 | bytes 262144 | tf_op jit(solution)/shard_map/concatenate | solution.py:375
  2.3 0.5 collective-permute-start
  2.9 4.1 %collective-permute-start.1 = (f32[2,16,128]{2,1,0:T(8,128)S(1)}, f32[2,16,128]{2,1,0:T(8,128)S(1)}, u32[]{:S(2)}, u32[]{:S(2)}) collective-permute-start(f32[2,16,128]{2,1,0:T(8,128)S(1)} %get-tuple-element.32), channel_id=1, source_target_pairs={{1,0},{2,1},{3,2},{4,3},{5,4},{6,5},{7,6},{0,7},{9,8},{10,9},{11,1... | collective-permute-start | bytes 49160 | tf_op jit(solution)/shard_map/ppermute | solution.py:302
  7.0 0.8 convert_element_type.14
  7.8 0.8 convert_element_type.12
  8.6 0.0 collective-permute-done.low
  8.7 0.0 collective-permute-done.1.high
  8.7 2.0 %collective-permute-start.2 = (f32[160,128]{1,0:T(8,128)S(1)}, f32[160,128]{1,0:T(8,128)S(1)}, u32[]{:S(2)}, u32[]{:S(2)}) collective-permute-start(f32[160,128]{1,0:T(8,128)S(1)} %pad_maximum_fusion.2), channel_id=1, source_target_pairs={{0,8},{8,16},{16,24},{24,0},{1,9},{9,17},{17,25},{25,1},{2,10},{10... | collective-permute-start | bytes 245768 | tf_op jit(solution)/shard_map/ppermute | solution.py:310
  10.7 1.0 %collective-permute-start.3 = (f32[160,128]{1,0:T(8,128)S(1)}, f32[160,128]{1,0:T(8,128)S(1)}, u32[]{:S(2)}, u32[]{:S(2)}) collective-permute-start(f32[160,128]{1,0:T(8,128)S(1)} %pad_maximum_fusion.3), channel_id=1, source_target_pairs={{8,0},{16,8},{24,16},{0,24},{9,1},{17,9},{25,17},{1,25},{10,2},{18... | collective-permute-start | bytes 245768 | tf_op jit(solution)/shard_map/ppermute | solution.py:311
  11.7 0.9 %pad_maximum_fusion.extra_ref = f32[24,2,8,128]{3,2,1,0:T(8,128)S(1)} fusion(f32[4,2,8,128]{3,2,1,0:T(8,128)S(1)} %convert_element_type.14, f32[8,2,8,128]{3,2,1,0:T(8,128)S(1)} %bitcast.45, f32[12,2,8,128]{3,2,1,0:T(8,128)} %bitcast.47), kind=kLoop, calls=%fused_computation | loop fusion | flops 98304 | bytes 393216 | tf_op jit(solution)/shard_map/concatenate | solution.py:377
  12.6 1.8 %collective-permute-done.2.down = f32[160,128]{1,0:T(8,128)S(1)} collective-permute-done((f32[160,128]{1,0:T(8,128)S(1)}, f32[160,128]{1,0:T(8,128)S(1)}, u32[]{:S(2)}, u32[]{:S(2)}) %collective-permute-start.2) | collective-permute-done | bytes 81952 | tf_op jit(solution)/shard_map/ppermute | solution.py:310
  14.4 1.7 %collective-permute-done.3.up = f32[160,128]{1,0:T(8,128)S(1)} collective-permute-done((f32[160,128]{1,0:T(8,128)S(1)}, f32[160,128]{1,0:T(8,128)S(1)}, u32[]{:S(2)}, u32[]{:S(2)}) %collective-permute-start.3) | collective-permute-done | bytes 81952 | tf_op jit(solution)/shard_map/ppermute | solution.py:311
  16.1 5.7 %shard_map.77 = (f32[3,4,2,8,128]{4,3,2,1,0:T(8,128)}, f32[2,12,8,128]{3,2,1,0:T(8,128)S(1)}, f32[2,16,128]{2,1,0:T(8,128)S(1)}, f32[2,16,128]{2,1,0:T(8,128)S(1...) custom-call(f32[24,2,8,128]{3,2,1,0:T(8,128)S(1)} %pad_maximum_fusion.extra_ref, ...), custom_call_target="tpu_custom_call" | custom-call | flops 26542080 | bytes 4194304 | tf_op jit(solution)/shard_map/pallas_call | solution.py:385
  21.8 0.0 collective-permute-start.4
  21.8 3.5 %collective-permute-start.5 = (f32[2,16,128]{2,1,0:T(8,128)S(1)}, f32[2,16,128]{2,1,0:T(8,128)S(1)}, u32[]{:S(2)}, u32[]{:S(2)}) collective-permute-start(f32[2,16,128]{2,1,0:T(8,128)S(1)} %get-tuple-element.37), channel_id=1, source_target_pairs={{1,0},{2,1},{3,2},{4,3},{5,4},{6,5},{7,6},{0,7},{9,8},{10,9},{11,1... | collective-permute-start | bytes 49160 | tf_op jit(solution)/shard_map/ppermute | solution.py:302
  25.3 1.4 %collective-permute-done.4.refs_4_ = f32[2,16,128]{2,1,0:T(8,128)S(1)} collective-permute-done((f32[2,16,128]{2,1,0:T(8,128)S(1)}, f32[2,16,128]{2,1,0:T(8,128)S(1)}, u32[]{:S(2)}, u32[]{:S(2)}) %collective-permute-start.4) | collective-permute-done | bytes 16416 | tf_op jit(solution)/shard_map/ppermute | solution.py:301
  26.8 0.0 collective-permute-done.5.refs_5_
  26.8 1.8 %collective-permute-start.6 = (f32[128,128]{1,0:T(8,128)S(1)}, f32[128,128]{1,0:T(8,128)S(1)}, u32[]{:S(2)}, u32[]{:S(2)}) collective-permute-start(f32[128,128]{1,0:T(8,128)S(1)} %pad_maximum_fusion.4), channel_id=1, source_target_pairs={{0,8},{8,16},{16,24},{24,0},{1,9},{9,17},{17,25},{25,1},{2,10},{10... | collective-permute-start | bytes 196616 | tf_op jit(solution)/shard_map/ppermute | solution.py:310
  28.6 1.2 %collective-permute-start.7 = (f32[128,128]{1,0:T(8,128)S(1)}, f32[128,128]{1,0:T(8,128)S(1)}, u32[]{:S(2)}, u32[]{:S(2)}) collective-permute-start(f32[128,128]{1,0:T(8,128)S(1)} %pad_maximum_fusion.5), channel_id=1, source_target_pairs={{8,0},{16,8},{24,16},{0,24},{9,1},{17,9},{25,17},{1,25},{10,2},{18... | collective-permute-start | bytes 196616 | tf_op jit(solution)/shard_map/ppermute | solution.py:311
  29.8 0.1 pad_add_fusion.refs_0_
  29.9 2.2 %collective-permute-done.6.refs_6_ = f32[128,128]{1,0:T(8,128)S(1)} collective-permute-done((f32[128,128]{1,0:T(8,128)S(1)}, f32[128,128]{1,0:T(8,128)S(1)}, u32[]{:S(2)}, u32[]{:S(2)}) %collective-permute-start.6) | collective-permute-done | bytes 65568 | tf_op jit(solution)/shard_map/ppermute | solution.py:310
  32.0 0.9 collective-permute-done.7.refs_7_
  32.9 5.5 %shard_map.78 = (f32[2,12,8,128]{3,2,1,0:T(8,128)S(1)}, f32[2,16,128]{2,1,0:T(8,128)S(1)}, f32[2,16,128]{2,1,0:T(8,128)S(1)}, f32[32,16,128]{2,1,0:T(8,128)}) custom-call(s32[4]{0:T(128)S(1)} %pad_add_fusion.refs_0_, bf16[54,8,16,128]{3,2,1,0:T(8,128)(2,1)S(1)} %get-tuple-element.33.refs_1_, f32[2,4,8,128]{3,2,1,0:T(8,128)S(1)} %get-tuple-element.34.refs_2_, ...), custom_call_target="tpu_custom_call" | custom-call | flops 26542080 | bytes 4194304 | tf_op jit(solution)/shard_map/pallas_call | solution.py:405
  38.4 3.9 %all-to-all-start = ((f32[32,16,128]{2,1,0:T(8,128)}), f32[32,16,128]{2,1,0:T(8,128)S(1)}, u32[]{:S(2)}, u32[]{:S(2)}) async-start(f32[32,16,128]{2,1,0:T(8,128)} %get-tuple-element.41), calls=%async_computation | async-start | bytes 524288 | tf_op jit(solution)/shard_map/all_to_all | solution.py:406
  42.3 2.7 %collective-permute-start.11 = (f32[96,128]{1,0:T(8,128)S(1)}, f32[96,128]{1,0:T(8,128)S(1)}, u32[]{:S(2)}, u32[]{:S(2)}) collective-permute-start(f32[96,128]{1,0:T(8,128)S(1)} %get-tuple-element.61), channel_id=1, source_target_pairs={{8,0},{16,8},{24,16},{0,24},{9,1},{17,9},{25,17},{1,25},{10,2},{18... | collective-permute-start | bytes 147464 | tf_op jit(solution)/shard_map/ppermute | solution.py:323
  45.0 0.0 collective-permute-start.10
  45.1 0.0 collective-permute-start.8
  45.1 3.5 %collective-permute-start.9 = (f32[2,16,128]{2,1,0:T(8,128)S(1)}, f32[2,16,128]{2,1,0:T(8,128)S(1)}, u32[]{:S(2)}, u32[]{:S(2)}) collective-permute-start(f32[2,16,128]{2,1,0:T(8,128)S(1)} %get-tuple-element.40), channel_id=1, source_target_pairs={{1,0},{2,1},{3,2},{4,3},{5,4},{6,5},{7,6},{0,7},{9,8},{10,9},{11,1... | collective-permute-start | bytes 49160 | tf_op jit(solution)/shard_map/ppermute | solution.py:319
  48.6 2.4 %collective-permute-done.8.refs_9_ = f32[2,16,128]{2,1,0:T(8,128)S(1)} collective-permute-done((f32[2,16,128]{2,1,0:T(8,128)S(1)}, f32[2,16,128]{2,1,0:T(8,128)S(1)}, u32[]{:S(2)}, u32[]{:S(2)}) %collective-permute-start.8) | collective-permute-done | bytes 16416 | tf_op jit(solution)/shard_map/ppermute | solution.py:318
  51.0 0.0 collective-permute-done.9.refs_10_
  51.0 0.0 collective-permute-done.11.refs_12_
  51.0 0.0 collective-permute-done.10.refs_11_
  51.0 1.3 %all-to-all-done.refs_13_ = f32[32,16,128]{2,1,0:T(8,128)S(1)} async-done(((f32[32,16,128]{2,1,0:T(8,128)}), f32[32,16,128]{2,1,0:T(8,128)S(1)}, u32[]{:S(2)}, u32[]{:S(2)}) %all-to-all-start) | async-done | bytes 262176 | tf_op jit(solution)/shard_map/all_to_all | solution.py:406
  52.3 5.6 %shard_map.79 = (f32[2,12,8,128]{3,2,1,0:T(8,128)S(1)}, f32[2,16,128]{2,1,0:T(8,128)S(1)}, f32[2,16,128]{2,1,0:T(8,128)S(1)}, f32[128,128]{1,0:T(8,128)S(1)}, f3...) custom-call(s32[4]{0:T(128)S(1)} %pad_add_fusion.refs_0_, ...), custom_call_target="tpu_custom_call" | custom-call | flops 26542080 | bytes 4194304 | tf_op jit(solution)/shard_map/pallas_call | solution.py:405
  57.9 4.0 %all-to-all-start.1 = ((f32[32,16,128]{2,1,0:T(8,128)}), f32[32,16,128]{2,1,0:T(8,128)S(1)}, u32[]{:S(2)}, u32[]{:S(2)}) async-start(f32[32,16,128]{2,1,0:T(8,128)} %get-tuple-element.50), calls=%async_computation.1 | async-start | bytes 524288 | tf_op jit(solution)/shard_map/all_to_all | solution.py:406
  61.9 2.7 %collective-permute-start.15 = (f32[96,128]{1,0:T(8,128)S(1)}, f32[96,128]{1,0:T(8,128)S(1)}, u32[]{:S(2)}, u32[]{:S(2)}) collective-permute-start(f32[96,128]{1,0:T(8,128)S(1)} %get-tuple-element.59), channel_id=1, source_target_pairs={{8,0},{16,8},{24,16},{0,24},{9,1},{17,9},{25,17},{1,25},{10,2},{18... | collective-permute-start | bytes 147464 | tf_op jit(solution)/shard_map/ppermute | solution.py:323
  64.7 0.0 collective-permute-start.14
  64.7 0.0 collective-permute-start.12
  64.7 3.5 %collective-permute-start.13 = (f32[2,16,128]{2,1,0:T(8,128)S(1)}, f32[2,16,128]{2,1,0:T(8,128)S(1)}, u32[]{:S(2)}, u32[]{:S(2)}) collective-permute-start(f32[2,16,128]{2,1,0:T(8,128)S(1)} %get-tuple-element.49), channel_id=1, source_target_pairs={{1,0},{2,1},{3,2},{4,3},{5,4},{6,5},{7,6},{0,7},{9,8},{10,9},{11,1... | collective-permute-start | bytes 49160 | tf_op jit(solution)/shard_map/ppermute | solution.py:319
  68.2 2.4 %collective-permute-done.12.refs_9_ = f32[2,16,128]{2,1,0:T(8,128)S(1)} collective-permute-done((f32[2,16,128]{2,1,0:T(8,128)S(1)}, f32[2,16,128]{2,1,0:T(8,128)S(1)}, u32[]{:S(2)}, u32[]{:S(2)}) %collective-permute-start.12) | collective-permute-done | bytes 16416 | tf_op jit(solution)/shard_map/ppermute | solution.py:318
  70.6 0.0 collective-permute-done.13.refs_10_
  70.6 0.0 collective-permute-done.15.refs_12_
  70.6 0.0 collective-permute-done.14.refs_11_
  70.6 1.3 %all-to-all-done.1.refs_13_ = f32[32,16,128]{2,1,0:T(8,128)S(1)} async-done(((f32[32,16,128]{2,1,0:T(8,128)}), f32[32,16,128]{2,1,0:T(8,128)S(1)}, u32[]{:S(2)}, u32[]{:S(2)}) %all-to-all-start.1) | async-done | bytes 262176 | tf_op jit(solution)/shard_map/all_to_all | solution.py:406
  71.9 4.7 %shard_map.80 = (f32[2,12,8,128]{3,2,1,0:T(8,128)S(1)}, f32[2,12,8,128]{3,2,1,0:T(8,128)S(1)}, f32[32,128]{1,0:T(8,128)S(1)}) custom-call(s32[4]{0:T(128)S(1)} %pad_add_fusion.refs_0_, bf16[54,8,16,128]{3,2,1,0:T(8,128)(2,1)S(1)} %get-tuple-element.33.refs_1_, f32[2,4,8,128]{3,2,1,0:T(8,128)S(1)} %get-tuple-element.34.refs_2_, ...), custom_call_target="tpu_custom_call" | custom-call | flops 26542080 | bytes 4194304 | tf_op jit(solution)/shard_map/pallas_call | solution.py:405
  76.7 11.0 %all_to_all.21 = f32[32,1,128]{2,1,0:T(1,128)S(1)} all-to-all(f32[32,1,128]{2,1,0:T(1,128)S(1)} %bitcast.44), channel_id=1, replica_groups=mesh['slab'=4,'sub'=8] {'slab','sub'}, dimensions={0} | all-to-all | bytes 32768 | tf_op jit(solution)/shard_map/all_to_all | solution.py:406
  87.6 0.8 shard_map.81
  (13 shorter events, 0.1 us)
Async XLA Ops:
  2.3 6.3 %collective-permute-start = (f32[2,16,128]{2,1,0:T(8,128)S(1)}, f32[2,16,128]{2,1,0:T(8,128)S(1)}, u32[]{:S(2)}, u32[]{:S(2)}) collective-permute-start(f32[2,16,128]{2,1,0:T(8,128)S(1)} %get-tuple-element.31), channel_id=1, source_target_pairs={{0,1},{1,2},{2,3},{3,4},{4,5},{5,6},{6,7},{7,0},{8,9},{9,10},{10,1... | collective-permute-start | bytes 49160 | tf_op jit(solution)/shard_map/ppermute | solution.py:301
  2.9 5.8 %collective-permute-start.1 = (f32[2,16,128]{2,1,0:T(8,128)S(1)}, f32[2,16,128]{2,1,0:T(8,128)S(1)}, u32[]{:S(2)}, u32[]{:S(2)}) collective-permute-start(f32[2,16,128]{2,1,0:T(8,128)S(1)} %get-tuple-element.32), channel_id=1, source_target_pairs={{1,0},{2,1},{3,2},{4,3},{5,4},{6,5},{7,6},{0,7},{9,8},{10,9},{11,1... | collective-permute-start | bytes 49160 | tf_op jit(solution)/shard_map/ppermute | solution.py:302
  8.7 5.7 %collective-permute-start.2 = (f32[160,128]{1,0:T(8,128)S(1)}, f32[160,128]{1,0:T(8,128)S(1)}, u32[]{:S(2)}, u32[]{:S(2)}) collective-permute-start(f32[160,128]{1,0:T(8,128)S(1)} %pad_maximum_fusion.2), channel_id=1, source_target_pairs={{0,8},{8,16},{16,24},{24,0},{1,9},{9,17},{17,25},{25,1},{2,10},{10... | collective-permute-start | bytes 245768 | tf_op jit(solution)/shard_map/ppermute | solution.py:310
  10.7 5.4 %collective-permute-start.3 = (f32[160,128]{1,0:T(8,128)S(1)}, f32[160,128]{1,0:T(8,128)S(1)}, u32[]{:S(2)}, u32[]{:S(2)}) collective-permute-start(f32[160,128]{1,0:T(8,128)S(1)} %pad_maximum_fusion.3), channel_id=1, source_target_pairs={{8,0},{16,8},{24,16},{0,24},{9,1},{17,9},{25,17},{1,25},{10,2},{18... | collective-permute-start | bytes 245768 | tf_op jit(solution)/shard_map/ppermute | solution.py:311
  21.8 5.0 %collective-permute-start.4 = (f32[2,16,128]{2,1,0:T(8,128)S(1)}, f32[2,16,128]{2,1,0:T(8,128)S(1)}, u32[]{:S(2)}, u32[]{:S(2)}) collective-permute-start(f32[2,16,128]{2,1,0:T(8,128)S(1)} %get-tuple-element.36), channel_id=1, source_target_pairs={{0,1},{1,2},{2,3},{3,4},{4,5},{5,6},{6,7},{7,0},{8,9},{9,10},{10,1... | collective-permute-start | bytes 49160 | tf_op jit(solution)/shard_map/ppermute | solution.py:301
  21.8 5.0 %collective-permute-start.5 = (f32[2,16,128]{2,1,0:T(8,128)S(1)}, f32[2,16,128]{2,1,0:T(8,128)S(1)}, u32[]{:S(2)}, u32[]{:S(2)}) collective-permute-start(f32[2,16,128]{2,1,0:T(8,128)S(1)} %get-tuple-element.37), channel_id=1, source_target_pairs={{1,0},{2,1},{3,2},{4,3},{5,4},{6,5},{7,6},{0,7},{9,8},{10,9},{11,1... | collective-permute-start | bytes 49160 | tf_op jit(solution)/shard_map/ppermute | solution.py:302
  26.8 5.2 %collective-permute-start.6 = (f32[128,128]{1,0:T(8,128)S(1)}, f32[128,128]{1,0:T(8,128)S(1)}, u32[]{:S(2)}, u32[]{:S(2)}) collective-permute-start(f32[128,128]{1,0:T(8,128)S(1)} %pad_maximum_fusion.4), channel_id=1, source_target_pairs={{0,8},{8,16},{16,24},{24,0},{1,9},{9,17},{17,25},{25,1},{2,10},{10... | collective-permute-start | bytes 196616 | tf_op jit(solution)/shard_map/ppermute | solution.py:310
  28.6 4.3 %collective-permute-start.7 = (f32[128,128]{1,0:T(8,128)S(1)}, f32[128,128]{1,0:T(8,128)S(1)}, u32[]{:S(2)}, u32[]{:S(2)}) collective-permute-start(f32[128,128]{1,0:T(8,128)S(1)} %pad_maximum_fusion.5), channel_id=1, source_target_pairs={{8,0},{16,8},{24,16},{0,24},{9,1},{17,9},{25,17},{1,25},{10,2},{18... | collective-permute-start | bytes 196616 | tf_op jit(solution)/shard_map/ppermute | solution.py:311
  38.4 14.0 %all-to-all-start = ((f32[32,16,128]{2,1,0:T(8,128)}), f32[32,16,128]{2,1,0:T(8,128)S(1)}, u32[]{:S(2)}, u32[]{:S(2)}) async-start(f32[32,16,128]{2,1,0:T(8,128)} %get-tuple-element.41), calls=%async_computation | async-start | bytes 524288 | tf_op jit(solution)/shard_map/all_to_all | solution.py:406
  42.3 8.7 %collective-permute-start.11 = (f32[96,128]{1,0:T(8,128)S(1)}, f32[96,128]{1,0:T(8,128)S(1)}, u32[]{:S(2)}, u32[]{:S(2)}) collective-permute-start(f32[96,128]{1,0:T(8,128)S(1)} %get-tuple-element.61), channel_id=1, source_target_pairs={{8,0},{16,8},{24,16},{0,24},{9,1},{17,9},{25,17},{1,25},{10,2},{18... | collective-permute-start | bytes 147464 | tf_op jit(solution)/shard_map/ppermute | solution.py:323
  45.0 6.0 %collective-permute-start.10 = (f32[96,128]{1,0:T(8,128)S(1)}, f32[96,128]{1,0:T(8,128)S(1)}, u32[]{:S(2)}, u32[]{:S(2)}) collective-permute-start(f32[96,128]{1,0:T(8,128)S(1)} %get-tuple-element.62), channel_id=1, source_target_pairs={{0,8},{8,16},{16,24},{24,0},{1,9},{9,17},{17,25},{25,1},{2,10},{10... | collective-permute-start | bytes 147464 | tf_op jit(solution)/shard_map/ppermute | solution.py:322
  45.1 5.9 %collective-permute-start.8 = (f32[2,16,128]{2,1,0:T(8,128)S(1)}, f32[2,16,128]{2,1,0:T(8,128)S(1)}, u32[]{:S(2)}, u32[]{:S(2)}) collective-permute-start(f32[2,16,128]{2,1,0:T(8,128)S(1)} %get-tuple-element.39), channel_id=1, source_target_pairs={{0,1},{1,2},{2,3},{3,4},{4,5},{5,6},{6,7},{7,0},{8,9},{9,10},{10,1... | collective-permute-start | bytes 49160 | tf_op jit(solution)/shard_map/ppermute | solution.py:318
  45.1 5.9 %collective-permute-start.9 = (f32[2,16,128]{2,1,0:T(8,128)S(1)}, f32[2,16,128]{2,1,0:T(8,128)S(1)}, u32[]{:S(2)}, u32[]{:S(2)}) collective-permute-start(f32[2,16,128]{2,1,0:T(8,128)S(1)} %get-tuple-element.40), channel_id=1, source_target_pairs={{1,0},{2,1},{3,2},{4,3},{5,4},{6,5},{7,6},{0,7},{9,8},{10,9},{11,1... | collective-permute-start | bytes 49160 | tf_op jit(solution)/shard_map/ppermute | solution.py:319
  57.9 14.0 %all-to-all-start.1 = ((f32[32,16,128]{2,1,0:T(8,128)}), f32[32,16,128]{2,1,0:T(8,128)S(1)}, u32[]{:S(2)}, u32[]{:S(2)}) async-start(f32[32,16,128]{2,1,0:T(8,128)} %get-tuple-element.50), calls=%async_computation.1 | async-start | bytes 524288 | tf_op jit(solution)/shard_map/all_to_all | solution.py:406
  61.9 8.7 %collective-permute-start.15 = (f32[96,128]{1,0:T(8,128)S(1)}, f32[96,128]{1,0:T(8,128)S(1)}, u32[]{:S(2)}, u32[]{:S(2)}) collective-permute-start(f32[96,128]{1,0:T(8,128)S(1)} %get-tuple-element.59), channel_id=1, source_target_pairs={{8,0},{16,8},{24,16},{0,24},{9,1},{17,9},{25,17},{1,25},{10,2},{18... | collective-permute-start | bytes 147464 | tf_op jit(solution)/shard_map/ppermute | solution.py:323
  64.7 6.0 %collective-permute-start.14 = (f32[96,128]{1,0:T(8,128)S(1)}, f32[96,128]{1,0:T(8,128)S(1)}, u32[]{:S(2)}, u32[]{:S(2)}) collective-permute-start(f32[96,128]{1,0:T(8,128)S(1)} %get-tuple-element.60), channel_id=1, source_target_pairs={{0,8},{8,16},{16,24},{24,0},{1,9},{9,17},{17,25},{25,1},{2,10},{10... | collective-permute-start | bytes 147464 | tf_op jit(solution)/shard_map/ppermute | solution.py:322
  64.7 5.9 %collective-permute-start.12 = (f32[2,16,128]{2,1,0:T(8,128)S(1)}, f32[2,16,128]{2,1,0:T(8,128)S(1)}, u32[]{:S(2)}, u32[]{:S(2)}) collective-permute-start(f32[2,16,128]{2,1,0:T(8,128)S(1)} %get-tuple-element.48), channel_id=1, source_target_pairs={{0,1},{1,2},{2,3},{3,4},{4,5},{5,6},{6,7},{7,0},{8,9},{9,10},{10,1... | collective-permute-start | bytes 49160 | tf_op jit(solution)/shard_map/ppermute | solution.py:318
  64.7 5.9 %collective-permute-start.13 = (f32[2,16,128]{2,1,0:T(8,128)S(1)}, f32[2,16,128]{2,1,0:T(8,128)S(1)}, u32[]{:S(2)}, u32[]{:S(2)}) collective-permute-start(f32[2,16,128]{2,1,0:T(8,128)S(1)} %get-tuple-element.49), channel_id=1, source_target_pairs={{1,0},{2,1},{3,2},{4,3},{5,4},{6,5},{7,6},{0,7},{9,8},{10,9},{11,1... | collective-permute-start | bytes 49160 | tf_op jit(solution)/shard_map/ppermute | solution.py:319
where the time goes:
time: 88.9 us; the launch traced here: 88.4 us
  starting transfers between devices  34.6 us (39%)
  Pallas kernels  22.3 us (25%)
  waiting for transfers between devices  15.3 us (17%)
  blocking collectives  11 us (12%)
  other arithmetic  4.28 us (5%)
    pallas_call x3, Pallas kernels, shards(): call(kernel, moved + outs, scratch, flops, 1, len(operands))(*operands)  15.8 us
    all_to_all x1, blocking collectives, shards(): peaks = lax.all_to_all(results[-1], ('slab', 'sub'), 0, 0, tiled=True)  11 us
    all_to_all x2, starting transfers between devices, shards(): peaks = lax.all_to_all(results[-1], ('slab', 'sub'), 0, 0, tiled=True)  7.94 us
    ppermute x2, starting transfers between devices, halo(): high = lax.ppermute(first_rows, 'sub', backward)  7.63 us
    ppermute x2, starting transfers between devices, near_halo(): high = lax.ppermute(first_rows, 'sub', backward)  7.08 us
    pallas_call x1, Pallas kernels, shards(): call(verlet_kernel, [velocities.shape, field, edge, edge, *pairs], [((pla...  5.73 us
    ppermute x2, starting transfers between devices, near_halo(): up = lax.ppermute(own[0].reshape(flat), 'slab', backward)  5.44 us
    ppermute x2, waiting for transfers between devices, near_halo(): low = lax.ppermute(last_rows, 'sub', forward)  4.79 us
  transfers between devices with their start and end apart: 18, of which 9 were waited for; matrix products, arithmetic and copies ran while one was open for 3% of the time, Pallas kernels for 0%

commit v1 on v0

--- a/solution.py
+++ b/solution.py
@@ -99,20 +99,35 @@
     return [(a, b, a >= bond_from and b <= bond_to) for a, b in zip(marks, marks[1:])]
 
 
-def sweep(slots, planes, own_tile, near, body):
+def plan(slots, planes):
+    counts, runs = {"own": 0, "edge": 0}, []
+    for plane in range(planes):
+        for first, last, bonded in cell_runs(slots):
+            part = "own" if 0 <= plane + first // 9 - 1 < planes else "edge"
+            runs.append((plane, first, last, bonded, part, counts[part]))
+            counts[part] += last - first
+    return runs, counts
+
+
+def sweep(slots, planes, parts, start, own_tile, near, body):
     totals = []
     for plane in range(planes):
         own = [own_tile(plane, c) for c in range(3 * slots)]
-        acc = [jnp.zeros_like(own[0]) for _ in range(3 * slots)]
-        for first, last, bonded in cell_runs(slots):
+        if start is None:
+            acc = [jnp.zeros_like(own[0]) for _ in range(3 * slots)]
+        else:
+            acc = [start[plane, c] for c in range(3 * slots)]
+        for at_plane, first, last, bonded, part, base in plan(slots, planes)[0]:
+            if at_plane != plane or part not in parts:
+                continue
             step_x = first // 9 - 1
             moved = [own[s] - step_x * cell_width for s in range(slots)] + own[slots:]
 
-            def step(cell, acc, moved=moved, bonded=bonded, plane=plane):
+            def step(cell, acc, moved=moved, bonded=bonded, plane=plane, part=part, base=base - first):
                 acc = list(acc)
                 for s2 in range(slots):
                     other = [near[plane * 9 + cell, c * slots + s2] for c in range(3)]
-                    each = body(plane, cell, s2, other, bonded)
+                    each = body(part, base + cell, plane, cell, s2, other, bonded)
                     for s1 in range(slots):
                         coef, sep = each(s1, [moved[c * slots + s1] for c in range(3)])
                         for c in range(3):
@@ -124,6 +139,17 @@
     return totals
 
 
+def fill_near(field, near, planes, channels, slots):
+    for plane in planes:
+        for c in range(channels):
+
+            def store(k, tile, plane=plane, c=c):
+                near[plane * 9 + k, c] = tile
+
+            main, lo, hi = field.plane(plane, c)
+            spread(main, lo, hi, c // slots == 1, c // slots == 2, store)
+
+
 def put_rows(low_ref, high_ref, plane, channel, tile):
     rows = tile.shape[0]
     low_ref[plane, pl.ds(channel, 1)] = tile[0:1]
@@ -139,25 +165,13 @@
             put_rows(low_ref, high_ref, plane, c, tile)
 
 
-def verlet_kernel(
-    extra_ref, own, low, high, down, up,
-    half_ref, next_ref, next_low, next_high, barrier_ref, weight_ref, near,
-):
-    _, slots, planes, rows, _ = half_ref.shape
-    vel_at, partner_at, anchor_at = 0, 3 * slots, 5 * slots
-    field = Field((own, low, high, down, up), planes, 4 * slots, rows)
-    for plane in range(planes + 2):
-        for c in range(4 * slots):
-
-            def store(k, tile, plane=plane, c=c):
-                near[plane * 9 + k, c] = tile
-
-            main, lo, hi = field.plane(plane, c)
-            spread(main, lo, hi, c // slots == 1, c // slots == 2, store)
-
-    def body(plane, cell, s2, other, bonded):
+def verlet_sums(slots, planes, part, start, extra_ref, own, barrier_ref, near):
+    partner_at = 3 * slots
+
+    def body(part, at, plane, cell, s2, other, bonded):
         label = near[plane * 9 + cell, 3 * slots + s2]
         alive = jnp.where(label < 0.0, dead_barrier, live_barrier)
+        pending = []
 
         def each(s1, mine):
             sep, dist_sq, coef = pair_terms(mine, other, alive)
@@ -171,14 +185,36 @@
             pending.append(barrier)
             if len(pending) == 2:
                 both = jnp.concatenate(pending, axis=0).astype(barrier_ref.dtype)
-                barrier_ref[plane * 27 + cell, (s2 * slots + s1) // 2] = both
+                barrier_ref[at, (s2 * slots + s1) // 2] = both
                 pending.clear()
             return coef, sep
 
         return each
 
-    pending = []
-    totals = sweep(slots, planes, lambda plane, c: own[plane, c], near, body)
+    return sweep(slots, planes, (part,), start, lambda plane, c: own[plane, c], near, body)
+
+
+def verlet_own_kernel(extra_ref, own, low, high, sum_ref, barrier_ref, near):
+    planes, channels, rows, _ = own.shape
+    slots = channels // 4
+    field = Field((own, low, high, None, None), planes, channels, rows)
+    fill_near(field, near, range(1, planes + 1), channels, slots)
+    totals = verlet_sums(slots, planes, "own", None, extra_ref, own, barrier_ref, near)
+    for plane in range(planes):
+        for c in range(3 * slots):
+            sum_ref[plane, c] = totals[plane][c]
+
+
+def verlet_edge_kernel(
+    extra_ref, own, down, up, sum_ref,
+    half_ref, next_ref, next_low, next_high, barrier_ref, weight_ref, near,
+):
+    planes, channels, rows, _ = own.shape
+    slots = channels // 4
+    vel_at, anchor_at = 0, 5 * slots
+    field = Field((own, None, None, down, up), planes, channels, rows)
+    fill_near(field, near, (0, planes + 1), channels, slots)
+    totals = verlet_sums(slots, planes, "edge", sum_ref, extra_ref, own, barrier_ref, near)
     for plane in range(planes):
         for s in range(slots):
             free = ((own[plane, 3 * slots + s] >= 0.0) & (extra_ref[anchor_at + s, plane] == 0.0)).astype(jnp.float32)
@@ -192,6 +228,36 @@
                 put_rows(next_low, next_high, plane, c, place)
 
 
+def descent_sums(slots, planes, parts, start, barriers, own, near):
+    def body(part, at, plane, cell, s2, other, bonded):
+        rows = other[0].shape[0]
+        both = [
+            barriers[part][at, (s2 * slots) // 2 + i].astype(jnp.float32) for i in range(slots // 2)
+        ]
+
+        def each(s1, mine):
+            barrier = both[s1 // 2][(s1 % 2) * rows : (s1 % 2 + 1) * rows]
+            sep, dist_sq, coef = pair_terms(mine, other, barrier)
+            if bonded:
+                coef += bond_coef(dist_sq, jnp.minimum(dead_barrier - barrier, 0.0))
+            return coef, sep
+
+        return each
+
+    return sweep(slots, planes, parts, start, lambda plane, c: own[plane, c], near, body)
+
+
+def descent_own_kernel(barrier_ref, own, low, high, sum_ref, near):
+    planes, channels, rows, _ = own.shape
+    slots = channels // 3
+    field = Field((own, low, high, None, None), planes, channels, rows)
+    fill_near(field, near, range(1, planes + 1), channels, slots)
+    totals = descent_sums(slots, planes, ("own",), None, {"own": barrier_ref}, own, near)
+    for plane in range(planes):
+        for c in range(channels):
+            sum_ref[plane, c] = totals[plane][c]
+
+
 def inverse_peak(peaks):
     peak_force = jnp.sqrt(jnp.max(jnp.max(peaks, axis=0, keepdims=True), axis=1, keepdims=True))
     return 1.0 / (peak_force + tiny_eps)
@@ -205,9 +271,14 @@
         del refs[:count]
         return taken
 
-    ids, barrier_ref, weight_ref = take(3)
+    ids, own_barrier, edge_barrier, weight_ref = take(4)
+    barriers = {"own": own_barrier, "edge": edge_barrier}
     places = take(5)
-    if moves:
+    if not moves:
+        (start,) = take(1)
+        parts, fill_planes = ("edge",), (0, planes + 1)
+    else:
+        start, parts, fill_planes = None, ("own", "edge"), range(planes + 2)
         own, low, high, down, up, mixed = take(6)
         now = take(1) + refs[-4:] if last else take(5)
         if last:
@@ -227,31 +298,8 @@
         force_ref, peak_ref, near = refs
     else:
         force_ref, force_low, force_high, mix_ref, near = refs
-    for plane in range(planes + 2):
-        for c in range(3 * slots):
-
-            def store(k, tile, plane=plane, c=c):
-                near[plane * 9 + k, c] = tile
-
-            main, lo, hi = field.plane(plane, c)
-            spread(main, lo, hi, c // slots == 1, c // slots == 2, store)
-
-    def body(plane, cell, s2, other, bonded):
-        both = [
-            barrier_ref[plane * 27 + cell, (s2 * slots) // 2 + i].astype(jnp.float32)
-            for i in range(slots // 2)
-        ]
-
-        def each(s1, mine):
-            barrier = both[s1 // 2][(s1 % 2) * rows : (s1 % 2 + 1) * rows]
-            sep, dist_sq, coef = pair_terms(mine, other, barrier)
-            if bonded:
-                coef += bond_coef(dist_sq, jnp.minimum(dead_barrier - barrier, 0.0))
-            return coef, sep
-
-        return each
-
-    totals = sweep(slots, planes, lambda plane, c: field.own[plane, c], near, body)
+    fill_near(field, near, fill_planes, 3 * slots, slots)
+    totals = descent_sums(slots, planes, parts, start, barriers, field.own, near)
     peak = None
     for plane in range(planes):
         forces = [total * weight_ref[plane, c % slots] for c, total in enumerate(totals[plane])]
@@ -295,11 +343,13 @@
     return forward, [(b, a) for a, b in forward]
 
 
-def halo(own, first_rows, last_rows):
+def row_halo(first_rows, last_rows):
+    forward, backward = ring("sub")
+    return lax.ppermute(last_rows, "sub", forward), lax.ppermute(first_rows, "sub", backward)
+
+
+def plane_halo(own, low, high):
     planes, channels, rows, lanes = own.shape
-    forward, backward = ring("sub")
-    low = lax.ppermute(last_rows, "sub", forward)
-    high = lax.ppermute(first_rows, "sub", backward)
 
     def packed(plane):
         return jnp.concatenate(
@@ -309,7 +359,7 @@
     forward, backward = ring("slab")
     down = lax.ppermute(packed(planes - 1), "slab", forward)
     up = lax.ppermute(packed(0), "slab", backward)
-    return (own, low, high, down, up)
+    return down, up
 
 
 def near_halo(own, first_rows, last_rows):
@@ -363,17 +413,17 @@
     field = (planes, 3 * slots, *tiles)
     edge = (planes, padded, lanes)
     near = ((planes + 2) * 9, 3 * slots, *tiles)
-    pairs = [
-        jax.ShapeDtypeStruct(
-            (planes * 27, slots * slots // 2, 2 * rows, lanes), jnp.bfloat16
-        ),
-        (planes, slots, *tiles),
-    ]
+    counts = plan(slots, planes)[1]
+    barrier = {
+        part: jax.ShapeDtypeStruct((count, slots * slots // 2, 2 * rows, lanes), jnp.bfloat16)
+        for part, count in counts.items()
+    }
+    share = {part: flops * count // (27 * planes) for part, count in counts.items()}
     ids = corner_devices()
     flat = offsets.reshape(3 * slots, planes, *tiles)
     labels = chain_label.astype(jnp.float32)
     wide = jnp.concatenate([flat, labels], axis=0)
-    start = halo(*call(prepare_kernel, [(planes, 4 * slots, *tiles), edge, edge])(wide))
+    wide, first, last = call(prepare_kernel, [(planes, 4 * slots, *tiles), edge, edge])(wide)
     extra = jnp.concatenate(
         [
             velocities.reshape(3 * slots, planes, *tiles),
@@ -382,13 +432,21 @@
         ],
         axis=0,
     )
-    half_velocity, place, first, last, *pairs = call(
-        verlet_kernel,
-        [velocities.shape, field, edge, edge, *pairs],
-        [((planes + 2) * 9, 4 * slots, *tiles)],
-        flops,
-    )(extra, *start)
-    places = halo(place, first, last)
+    near_wide = ((planes + 2) * 9, 4 * slots, *tiles)
+    low, high = row_halo(first, last)
+    sums, own_barrier = call(
+        verlet_own_kernel, [field, barrier["own"]], [near_wide], share["own"]
+    )(extra, wide, low, high)
+    down, up = plane_halo(wide, low, high)
+    half_velocity, place, first, last, edge_barrier, weight = call(
+        verlet_edge_kernel,
+        [velocities.shape, field, edge, edge, barrier["edge"], (planes, slots, *tiles)],
+        [near_wide],
+        share["edge"],
+    )(extra, wide, down, up, sums)
+    low, high = row_halo(first, last)
+    (sums,) = call(descent_own_kernel, [field], [near], share["own"])(own_barrier, place, low, high)
+    places = (place, low, high, *plane_halo(place, low, high))
     moves = ()
     for descent in range(DESCENTS):
         final = descent + 1 == DESCENTS
@@ -401,7 +459,7 @@
         scratch = [near]
         if final:
             moved, scratch = moved[:1], scratch + moved[1:]
-        operands = (ids, *pairs, *places, *moves)
+        operands = (ids, own_barrier, edge_barrier, weight, *places, *(moves or (sums,)))
         results = call(kernel, moved + outs, scratch, flops, 1, len(operands))(*operands)
         peaks = lax.all_to_all(results[-1], ("slab", "sub"), 0, 0, tiled=True)
         if final:

time: 88.9 us -> 82.9 us (0.933)
  waiting for transfers between devices: 15.3 us -> 10.1 us
    ppermute x8, waiting for transfers between devices: 7.91 us -> 2.64 us  [the longest x2 1.43 us: row_halo(): lax.ppermute(last_rows, 'sub', forward)]
    pallas_call x1 -> x3, Pallas kernels: 5.73 us -> 8.53 us  [the longest x1 3.42 us: shards(): call(verlet_own_kernel, [field, barrier['own']], [near_wide], share['own'])]
    pallas_call x3, Pallas kernels: 15.8 us -> 13.2 us  [shards(): call(kernel, moved + outs, scratch, flops, 1, len(operands))(*operands)]
    concatenate x1, other arithmetic: 0.91 us -> 0.01 us  [shards(): jnp.concatenate([velocities.reshape(3 * slots, planes, *tiles), partners....]
  transfers between devices with their start and end apart: 18 -> 18, of which waited for: 9 -> 7; matrix products, arithmetic and copies ran while one was open for 3% -> 2% of each run, Pallas kernels for 0% -> 7%
where the time goes in v1:
time: 82.9 us; the launch traced here: 82.5 us
  starting transfers between devices  34.6 us (42%)
  Pallas kernels  22.5 us (27%)
  blocking collectives  11 us (13%)
  waiting for transfers between devices  10.1 us (12%)
  other arithmetic  3.42 us (4%)
  between operations  0.84 us (1%)
    pallas_call x3, Pallas kernels, shards(): call(kernel, moved + outs, scratch, flops, 1, len(operands))(*operands)  13.2 us
    all_to_all x1, blocking collectives, shards(): peaks = lax.all_to_all(results[-1], ('slab', 'sub'), 0, 0, tiled=True)  11 us
    all_to_all x2, starting transfers between devices, shards(): peaks = lax.all_to_all(results[-1], ('slab', 'sub'), 0, 0, tiled=True)  7.94 us
    ppermute x2, starting transfers between devices, row_halo(): lax.ppermute(first_rows, 'sub', backward)  7.63 us
    ppermute x2, starting transfers between devices, near_halo(): high = lax.ppermute(first_rows, 'sub', backward)  7.08 us
    ppermute x2, starting transfers between devices, near_halo(): up = lax.ppermute(own[0].reshape(flat), 'slab', backward)  5.44 us
    ppermute x2, waiting for transfers between devices, near_halo(): low = lax.ppermute(last_rows, 'sub', forward)  4.79 us
    ppermute x2, starting transfers between devices, plane_halo(): down = lax.ppermute(packed(planes - 1), 'slab', forward)  3.8 us
  transfers between devices with their start and end apart: 18, of which 7 were waited for; matrix products, arithmetic and copies ran while one was open for 2% of the time, Pallas kernels for 7%

profile of v1, /device:TPU:0, one launch (start us, length us, event | category | flops | bytes accessed | tf_op | source)
XLA Modules:
  0.0 82.5 jit_solution(4142633481942985116)
XLA Ops:
  0.6 0.0 copy-start
  0.6 0.8 convert_element_type.15
  1.4 0.9 %pad_maximum_fusion.1.wide_ref = f32[16,2,8,128]{3,2,1,0:T(8,128)S(1)} fusion(f32[4,2,8,128]{3,2,1,0:T(8,128)S(1)} %convert_element_type.15, f32[12,2,8,128]{3,2,1,0:T(8,128)} %bitcast.46), kind=kLoop, calls=%fused_computation.1 | loop fusion | flops 32768 | bytes 262144 | tf_op jit(solution)/shard_map/concatenate | solution.py:425
  2.4 0.5 collective-permute-start
  2.9 4.1 %collective-permute-start.1 = (f32[2,16,128]{2,1,0:T(8,128)S(1)}, f32[2,16,128]{2,1,0:T(8,128)S(1)}, u32[]{:S(2)}, u32[]{:S(2)}) collective-permute-start(f32[2,16,128]{2,1,0:T(8,128)S(1)} %get-tuple-element.34), channel_id=1, source_target_pairs={{1,0},{2,1},{3,2},{4,3},{5,4},{6,5},{7,6},{0,7},{9,8},{10,9},{11,1... | collective-permute-start | bytes 49160 | tf_op jit(solution)/shard_map/ppermute | solution.py:348
  7.1 0.8 convert_element_type.14
  7.8 0.8 %convert_element_type.12 = f32[2,4,2,8,128]{4,3,2,1,0:T(8,128)S(1)} convert(s32[2,4,2,8,128]{4,3,2,1,0:T(8,128)} %param.8) | non-fusion elementwise | flops 16384 | bytes 131072 | tf_op jit(solution)/shard_map/convert_element_type | solution.py:430
  8.7 0.0 collective-permute-done.low
  8.7 0.0 collective-permute-done.1.high
  8.7 2.0 %collective-permute-start.2 = (f32[160,128]{1,0:T(8,128)S(1)}, f32[160,128]{1,0:T(8,128)S(1)}, u32[]{:S(2)}, u32[]{:S(2)}) collective-permute-start(f32[160,128]{1,0:T(8,128)S(1)} %pad_maximum_fusion.2), channel_id=1, source_target_pairs={{0,8},{8,16},{16,24},{24,0},{1,9},{9,17},{17,25},{25,1},{2,10},{10... | collective-permute-start | bytes 245768 | tf_op jit(solution)/shard_map/ppermute | solution.py:360
  10.7 1.0 %collective-permute-start.3 = (f32[160,128]{1,0:T(8,128)S(1)}, f32[160,128]{1,0:T(8,128)S(1)}, u32[]{:S(2)}, u32[]{:S(2)}) collective-permute-start(f32[160,128]{1,0:T(8,128)S(1)} %pad_maximum_fusion.3), channel_id=1, source_target_pairs={{8,0},{16,8},{24,16},{0,24},{9,1},{17,9},{25,17},{1,25},{10,2},{18... | collective-permute-start | bytes 245768 | tf_op jit(solution)/shard_map/ppermute | solution.py:361
  11.8 0.0 copy-done
  11.8 3.4 %shard_map.77 = (f32[2,12,8,128]{3,2,1,0:T(8,128)S(1)}, bf16[36,8,16,128]{3,2,1,0:T(8,128)(2,1)S(1)}) custom-call(f32[24,2,8,128]{3,2,1,0:T(8,128)S(1)} %pad_maximum_fusion.extra_ref, f32[2,16,8,128]{3,2,1,0:T(8,128)S(1)} %get-tuple-element.32.own, f32[2,16,128]{2,1,0:T(8,128)S(1)} %collective-permute-done.low, f32[2,16,128]{2,1,0:T(8,128)S(1)} %collective-permute-done.1.high), custom_call_target="tpu_custom_call" | custom-call | flops 17694720 | bytes 4194304 | tf_op jit(solution)/shard_map/pallas_call | solution.py:437
  15.2 0.0 collective-permute-done.2.down
  15.2 0.9 %collective-permute-done.3.up = f32[160,128]{1,0:T(8,128)S(1)} collective-permute-done((f32[160,128]{1,0:T(8,128)S(1)}, f32[160,128]{1,0:T(8,128)S(1)}, u32[]{:S(2)}, u32[]{:S(2)}) %collective-permute-start.3) | collective-permute-done | bytes 81952 | tf_op jit(solution)/shard_map/ppermute | solution.py:361
  16.1 2.4 %shard_map.78 = (f32[3,4,2,8,128]{4,3,2,1,0:T(8,128)}, f32[2,12,8,128]{3,2,1,0:T(8,128)S(1)}, f32[2,16,128]{2,1,0:T(8,128)S(1)}, f32[2,16,128]{2,1,0:T(8,128)S(1...) custom-call(f32[24,2,8,128]{3,2,1,0:T(8,128)S(1)} %pad_maximum_fusion.extra_ref, ...), custom_call_target="tpu_custom_call" | custom-call | flops 8847360 | bytes 4194304 | tf_op jit(solution)/shard_map/pallas_call | solution.py:441
  18.5 0.0 collective-permute-start.4
  18.5 3.5 %collective-permute-start.5 = (f32[2,16,128]{2,1,0:T(8,128)S(1)}, f32[2,16,128]{2,1,0:T(8,128)S(1)}, u32[]{:S(2)}, u32[]{:S(2)}) collective-permute-start(f32[2,16,128]{2,1,0:T(8,128)S(1)} %get-tuple-element.41), channel_id=1, source_target_pairs={{1,0},{2,1},{3,2},{4,3},{5,4},{6,5},{7,6},{0,7},{9,8},{10,9},{11,1... | collective-permute-start | bytes 49160 | tf_op jit(solution)/shard_map/ppermute | solution.py:348
  22.1 1.4 %collective-permute-done.4.low.refs_5_ = f32[2,16,128]{2,1,0:T(8,128)S(1)} collective-permute-done((f32[2,16,128]{2,1,0:T(8,128)S(1)}, f32[2,16,128]{2,1,0:T(8,128)S(1)}, u32[]{:S(2)}, u32[]{:S(2)}) %collective-permute-start.4) | collective-permute-done | bytes 16416 | tf_op jit(solution)/shard_map/ppermute | solution.py:348
  23.5 0.0 collective-permute-done.5.high.refs_6_
  23.5 1.8 %collective-permute-start.6 = (f32[128,128]{1,0:T(8,128)S(1)}, f32[128,128]{1,0:T(8,128)S(1)}, u32[]{:S(2)}, u32[]{:S(2)}) collective-permute-start(f32[128,128]{1,0:T(8,128)S(1)} %pad_maximum_fusion.4), channel_id=1, source_target_pairs={{0,8},{8,16},{16,24},{24,0},{1,9},{9,17},{17,25},{25,1},{2,10},{10... | collective-permute-start | bytes 196616 | tf_op jit(solution)/shard_map/ppermute | solution.py:360
  25.3 1.2 %collective-permute-start.7 = (f32[128,128]{1,0:T(8,128)S(1)}, f32[128,128]{1,0:T(8,128)S(1)}, u32[]{:S(2)}, u32[]{:S(2)}) collective-permute-start(f32[128,128]{1,0:T(8,128)S(1)} %pad_maximum_fusion.5), channel_id=1, source_target_pairs={{8,0},{16,8},{24,16},{0,24},{9,1},{17,9},{25,17},{1,25},{10,2},{18... | collective-permute-start | bytes 196616 | tf_op jit(solution)/shard_map/ppermute | solution.py:361
  26.5 0.1 pad_add_fusion.refs_0_
  26.6 2.7 %shard_map.79.refs_9_ = f32[2,12,8,128]{3,2,1,0:T(8,128)S(1)} custom-call(bf16[36,8,16,128]{3,2,1,0:T(8,128)(2,1)S(1)} %get-tuple-element.35.barrier_ref.refs_1_, f32[2,12,8,128]{3,2,1,0:T(8,128)S(1)} %get-tuple-element.39.own.refs_4_, f32[2,16,128]{2,1,0:T(8,128)S(1)} %collective-permute-done.4.low.refs_5_, ...), custom_call_target="tpu_custom_call" | custom-call | flops 17694720 | bytes 4194304 | tf_op jit(solution)/shard_map/pallas_call | solution.py:448
  29.3 0.0 collective-permute-done.6.refs_7_
  29.3 0.3 collective-permute-done.7.refs_8_
  29.6 2.8 %shard_map.80 = (f32[2,12,8,128]{3,2,1,0:T(8,128)S(1)}, f32[2,16,128]{2,1,0:T(8,128)S(1)}, f32[2,16,128]{2,1,0:T(8,128)S(1)}, f32[32,16,128]{2,1,0:T(8,128)}) custom-call(s32[4]{0:T(128)S(1)} %pad_add_fusion.refs_0_, bf16[36,8,16,128]{3,2,1,0:T(8,128)(2,1)S(1)} %get-tuple-element.35.barrier_ref.refs_1_, ...), custom_call_target="tpu_custom_call" | custom-call | flops 26542080 | bytes 4194304 | tf_op jit(solution)/shard_map/pallas_call | solution.py:463
  32.5 3.9 %all-to-all-start = ((f32[32,16,128]{2,1,0:T(8,128)}), f32[32,16,128]{2,1,0:T(8,128)S(1)}, u32[]{:S(2)}, u32[]{:S(2)}) async-start(f32[32,16,128]{2,1,0:T(8,128)} %get-tuple-element.45), calls=%async_computation | async-start | bytes 524288 | tf_op jit(solution)/shard_map/all_to_all | solution.py:464
  36.4 2.7 %collective-permute-start.11 = (f32[96,128]{1,0:T(8,128)S(1)}, f32[96,128]{1,0:T(8,128)S(1)}, u32[]{:S(2)}, u32[]{:S(2)}) collective-permute-start(f32[96,128]{1,0:T(8,128)S(1)} %get-tuple-element.65), channel_id=1, source_target_pairs={{8,0},{16,8},{24,16},{0,24},{9,1},{17,9},{25,17},{1,25},{10,2},{18... | collective-permute-start | bytes 147464 | tf_op jit(solution)/shard_map/ppermute | solution.py:373
  39.1 0.0 collective-permute-start.10
  39.1 0.0 collective-permute-start.8
  39.1 3.5 %collective-permute-start.9 = (f32[2,16,128]{2,1,0:T(8,128)S(1)}, f32[2,16,128]{2,1,0:T(8,128)S(1)}, u32[]{:S(2)}, u32[]{:S(2)}) collective-permute-start(f32[2,16,128]{2,1,0:T(8,128)S(1)} %get-tuple-element.44), channel_id=1, source_target_pairs={{1,0},{2,1},{3,2},{4,3},{5,4},{6,5},{7,6},{0,7},{9,8},{10,9},{11,1... | collective-permute-start | bytes 49160 | tf_op jit(solution)/shard_map/ppermute | solution.py:369
  42.7 2.4 %collective-permute-done.8.refs_10_ = f32[2,16,128]{2,1,0:T(8,128)S(1)} collective-permute-done((f32[2,16,128]{2,1,0:T(8,128)S(1)}, f32[2,16,128]{2,1,0:T(8,128)S(1)}, u32[]{:S(2)}, u32[]{:S(2)}) %collective-permute-start.8) | collective-permute-done | bytes 16416 | tf_op jit(solution)/shard_map/ppermute | solution.py:368
  45.1 0.0 collective-permute-done.9.refs_11_
  45.1 0.0 collective-permute-done.11.refs_13_
  45.1 0.0 collective-permute-done.10.refs_12_
  45.1 1.3 %all-to-all-done.refs_14_ = f32[32,16,128]{2,1,0:T(8,128)S(1)} async-done(((f32[32,16,128]{2,1,0:T(8,128)}), f32[32,16,128]{2,1,0:T(8,128)S(1)}, u32[]{:S(2)}, u32[]{:S(2)}) %all-to-all-start) | async-done | bytes 262176 | tf_op jit(solution)/shard_map/all_to_all | solution.py:464
  46.4 5.6 %shard_map.81 = (f32[2,12,8,128]{3,2,1,0:T(8,128)S(1)}, f32[2,16,128]{2,1,0:T(8,128)S(1)}, f32[2,16,128]{2,1,0:T(8,128)S(1)}, f32[128,128]{1,0:T(8,128)S(1)}, f3...) custom-call(s32[4]{0:T(128)S(1)} %pad_add_fusion.refs_0_, ...), custom_call_target="tpu_custom_call" | custom-call | flops 26542080 | bytes 4194304 | tf_op jit(solution)/shard_map/pallas_call | solution.py:463
  52.0 4.0 %all-to-all-start.1 = ((f32[32,16,128]{2,1,0:T(8,128)}), f32[32,16,128]{2,1,0:T(8,128)S(1)}, u32[]{:S(2)}, u32[]{:S(2)}) async-start(f32[32,16,128]{2,1,0:T(8,128)} %get-tuple-element.54), calls=%async_computation.1 | async-start | bytes 524288 | tf_op jit(solution)/shard_map/all_to_all | solution.py:464
  56.0 2.7 %collective-permute-start.15 = (f32[96,128]{1,0:T(8,128)S(1)}, f32[96,128]{1,0:T(8,128)S(1)}, u32[]{:S(2)}, u32[]{:S(2)}) collective-permute-start(f32[96,128]{1,0:T(8,128)S(1)} %get-tuple-element.63), channel_id=1, source_target_pairs={{8,0},{16,8},{24,16},{0,24},{9,1},{17,9},{25,17},{1,25},{10,2},{18... | collective-permute-start | bytes 147464 | tf_op jit(solution)/shard_map/ppermute | solution.py:373
  58.8 0.0 collective-permute-start.14
  58.8 0.0 collective-permute-start.12
  58.8 3.5 %collective-permute-start.13 = (f32[2,16,128]{2,1,0:T(8,128)S(1)}, f32[2,16,128]{2,1,0:T(8,128)S(1)}, u32[]{:S(2)}, u32[]{:S(2)}) collective-permute-start(f32[2,16,128]{2,1,0:T(8,128)S(1)} %get-tuple-element.53), channel_id=1, source_target_pairs={{1,0},{2,1},{3,2},{4,3},{5,4},{6,5},{7,6},{0,7},{9,8},{10,9},{11,1... | collective-permute-start | bytes 49160 | tf_op jit(solution)/shard_map/ppermute | solution.py:369
  62.3 2.4 %collective-permute-done.12.refs_10_ = f32[2,16,128]{2,1,0:T(8,128)S(1)} collective-permute-done((f32[2,16,128]{2,1,0:T(8,128)S(1)}, f32[2,16,128]{2,1,0:T(8,128)S(1)}, u32[]{:S(2)}, u32[]{:S(2)}) %collective-permute-start.12) | collective-permute-done | bytes 16416 | tf_op jit(solution)/shard_map/ppermute | solution.py:368
  64.7 0.0 collective-permute-done.13.refs_11_
  64.7 0.0 collective-permute-done.15.refs_13_
  64.7 0.0 collective-permute-done.14.refs_12_
  64.7 1.3 %all-to-all-done.1.refs_14_ = f32[32,16,128]{2,1,0:T(8,128)S(1)} async-done(((f32[32,16,128]{2,1,0:T(8,128)}), f32[32,16,128]{2,1,0:T(8,128)S(1)}, u32[]{:S(2)}, u32[]{:S(2)}) %all-to-all-start.1) | async-done | bytes 262176 | tf_op jit(solution)/shard_map/all_to_all | solution.py:464
  66.0 4.7 %shard_map.82 = (f32[2,12,8,128]{3,2,1,0:T(8,128)S(1)}, f32[2,12,8,128]{3,2,1,0:T(8,128)S(1)}, f32[32,128]{1,0:T(8,128)S(1)}) custom-call(s32[4]{0:T(128)S(1)} %pad_add_fusion.refs_0_, bf16[36,8,16,128]{3,2,1,0:T(8,128)(2,1)S(1)} %get-tuple-element.35.barrier_ref.refs_1_, bf16[18,8,16,128]{3,2,1,0:T(8,128)(2,1)S(1)} %get-tuple-element.37.refs_2_, ...), custom_call_target="tpu_custom_call" | custom-call | flops 26542080 | bytes 4194304 | tf_op jit(solution)/shard_map/pallas_call | solution.py:463
  70.7 11.0 %all_to_all.21 = f32[32,1,128]{2,1,0:T(1,128)S(1)} all-to-all(f32[32,1,128]{2,1,0:T(1,128)S(1)} %bitcast.44), channel_id=1, replica_groups=mesh['slab'=4,'sub'=8] {'slab','sub'}, dimensions={0} | all-to-all | bytes 32768 | tf_op jit(solution)/shard_map/all_to_all | solution.py:464
  81.7 0.8 shard_map.83
  (14 shorter events, 0.1 us)
Async XLA Ops:
  0.6 11.1 %copy-start = (f32[3,4,2,8,128]{4,3,2,1,0:T(8,128)S(1)}, f32[3,4,2,8,128]{4,3,2,1,0:T(8,128)}, u32[]{:S(2)}) copy-start(f32[3,4,2,8,128]{4,3,2,1,0:T(8,128)} %param.6) | copy-start | bytes 294916
  2.4 6.3 %collective-permute-start = (f32[2,16,128]{2,1,0:T(8,128)S(1)}, f32[2,16,128]{2,1,0:T(8,128)S(1)}, u32[]{:S(2)}, u32[]{:S(2)}) collective-permute-start(f32[2,16,128]{2,1,0:T(8,128)S(1)} %get-tuple-element.33), channel_id=1, source_target_pairs={{0,1},{1,2},{2,3},{3,4},{4,5},{5,6},{6,7},{7,0},{8,9},{9,10},{10,1... | collective-permute-start | bytes 49160 | tf_op jit(solution)/shard_map/ppermute | solution.py:348
  2.9 5.8 %collective-permute-start.1 = (f32[2,16,128]{2,1,0:T(8,128)S(1)}, f32[2,16,128]{2,1,0:T(8,128)S(1)}, u32[]{:S(2)}, u32[]{:S(2)}) collective-permute-start(f32[2,16,128]{2,1,0:T(8,128)S(1)} %get-tuple-element.34), channel_id=1, source_target_pairs={{1,0},{2,1},{3,2},{4,3},{5,4},{6,5},{7,6},{0,7},{9,8},{10,9},{11,1... | collective-permute-start | bytes 49160 | tf_op jit(solution)/shard_map/ppermute | solution.py:348
  8.7 6.5 %collective-permute-start.2 = (f32[160,128]{1,0:T(8,128)S(1)}, f32[160,128]{1,0:T(8,128)S(1)}, u32[]{:S(2)}, u32[]{:S(2)}) collective-permute-start(f32[160,128]{1,0:T(8,128)S(1)} %pad_maximum_fusion.2), channel_id=1, source_target_pairs={{0,8},{8,16},{16,24},{24,0},{1,9},{9,17},{17,25},{25,1},{2,10},{10... | collective-permute-start | bytes 245768 | tf_op jit(solution)/shard_map/ppermute | solution.py:360
  10.7 5.4 %collective-permute-start.3 = (f32[160,128]{1,0:T(8,128)S(1)}, f32[160,128]{1,0:T(8,128)S(1)}, u32[]{:S(2)}, u32[]{:S(2)}) collective-permute-start(f32[160,128]{1,0:T(8,128)S(1)} %pad_maximum_fusion.3), channel_id=1, source_target_pairs={{8,0},{16,8},{24,16},{0,24},{9,1},{17,9},{25,17},{1,25},{10,2},{18... | collective-permute-start | bytes 245768 | tf_op jit(solution)/shard_map/ppermute | solution.py:361
  18.5 5.0 %collective-permute-start.4 = (f32[2,16,128]{2,1,0:T(8,128)S(1)}, f32[2,16,128]{2,1,0:T(8,128)S(1)}, u32[]{:S(2)}, u32[]{:S(2)}) collective-permute-start(f32[2,16,128]{2,1,0:T(8,128)S(1)} %get-tuple-element.40), channel_id=1, source_target_pairs={{0,1},{1,2},{2,3},{3,4},{4,5},{5,6},{6,7},{7,0},{8,9},{9,10},{10,1... | collective-permute-start | bytes 49160 | tf_op jit(solution)/shard_map/ppermute | solution.py:348
  18.5 5.0 %collective-permute-start.5 = (f32[2,16,128]{2,1,0:T(8,128)S(1)}, f32[2,16,128]{2,1,0:T(8,128)S(1)}, u32[]{:S(2)}, u32[]{:S(2)}) collective-permute-start(f32[2,16,128]{2,1,0:T(8,128)S(1)} %get-tuple-element.41), channel_id=1, source_target_pairs={{1,0},{2,1},{3,2},{4,3},{5,4},{6,5},{7,6},{0,7},{9,8},{10,9},{11,1... | collective-permute-start | bytes 49160 | tf_op jit(solution)/shard_map/ppermute | solution.py:348
  23.5 5.8 %collective-permute-start.6 = (f32[128,128]{1,0:T(8,128)S(1)}, f32[128,128]{1,0:T(8,128)S(1)}, u32[]{:S(2)}, u32[]{:S(2)}) collective-permute-start(f32[128,128]{1,0:T(8,128)S(1)} %pad_maximum_fusion.4), channel_id=1, source_target_pairs={{0,8},{8,16},{16,24},{24,0},{1,9},{9,17},{17,25},{25,1},{2,10},{10... | collective-permute-start | bytes 196616 | tf_op jit(solution)/shard_map/ppermute | solution.py:360
  25.3 4.3 %collective-permute-start.7 = (f32[128,128]{1,0:T(8,128)S(1)}, f32[128,128]{1,0:T(8,128)S(1)}, u32[]{:S(2)}, u32[]{:S(2)}) collective-permute-start(f32[128,128]{1,0:T(8,128)S(1)} %pad_maximum_fusion.5), channel_id=1, source_target_pairs={{8,0},{16,8},{24,16},{0,24},{9,1},{17,9},{25,17},{1,25},{10,2},{18... | collective-permute-start | bytes 196616 | tf_op jit(solution)/shard_map/ppermute | solution.py:361
  32.5 14.0 %all-to-all-start = ((f32[32,16,128]{2,1,0:T(8,128)}), f32[32,16,128]{2,1,0:T(8,128)S(1)}, u32[]{:S(2)}, u32[]{:S(2)}) async-start(f32[32,16,128]{2,1,0:T(8,128)} %get-tuple-element.45), calls=%async_computation | async-start | bytes 524288 | tf_op jit(solution)/shard_map/all_to_all | solution.py:464
  36.4 8.7 %collective-permute-start.11 = (f32[96,128]{1,0:T(8,128)S(1)}, f32[96,128]{1,0:T(8,128)S(1)}, u32[]{:S(2)}, u32[]{:S(2)}) collective-permute-start(f32[96,128]{1,0:T(8,128)S(1)} %get-tuple-element.65), channel_id=1, source_target_pairs={{8,0},{16,8},{24,16},{0,24},{9,1},{17,9},{25,17},{1,25},{10,2},{18... | collective-permute-start | bytes 147464 | tf_op jit(solution)/shard_map/ppermute | solution.py:373
  39.1 6.0 %collective-permute-start.10 = (f32[96,128]{1,0:T(8,128)S(1)}, f32[96,128]{1,0:T(8,128)S(1)}, u32[]{:S(2)}, u32[]{:S(2)}) collective-permute-start(f32[96,128]{1,0:T(8,128)S(1)} %get-tuple-element.66), channel_id=1, source_target_pairs={{0,8},{8,16},{16,24},{24,0},{1,9},{9,17},{17,25},{25,1},{2,10},{10... | collective-permute-start | bytes 147464 | tf_op jit(solution)/shard_map/ppermute | solution.py:372
  39.1 5.9 %collective-permute-start.8 = (f32[2,16,128]{2,1,0:T(8,128)S(1)}, f32[2,16,128]{2,1,0:T(8,128)S(1)}, u32[]{:S(2)}, u32[]{:S(2)}) collective-permute-start(f32[2,16,128]{2,1,0:T(8,128)S(1)} %get-tuple-element.43), channel_id=1, source_target_pairs={{0,1},{1,2},{2,3},{3,4},{4,5},{5,6},{6,7},{7,0},{8,9},{9,10},{10,1... | collective-permute-start | bytes 49160 | tf_op jit(solution)/shard_map/ppermute | solution.py:368
  39.1 5.9 %collective-permute-start.9 = (f32[2,16,128]{2,1,0:T(8,128)S(1)}, f32[2,16,128]{2,1,0:T(8,128)S(1)}, u32[]{:S(2)}, u32[]{:S(2)}) collective-permute-start(f32[2,16,128]{2,1,0:T(8,128)S(1)} %get-tuple-element.44), channel_id=1, source_target_pairs={{1,0},{2,1},{3,2},{4,3},{5,4},{6,5},{7,6},{0,7},{9,8},{10,9},{11,1... | collective-permute-start | bytes 49160 | tf_op jit(solution)/shard_map/ppermute | solution.py:369
  52.0 14.0 %all-to-all-start.1 = ((f32[32,16,128]{2,1,0:T(8,128)}), f32[32,16,128]{2,1,0:T(8,128)S(1)}, u32[]{:S(2)}, u32[]{:S(2)}) async-start(f32[32,16,128]{2,1,0:T(8,128)} %get-tuple-element.54), calls=%async_computation.1 | async-start | bytes 524288 | tf_op jit(solution)/shard_map/all_to_all | solution.py:464
  56.0 8.7 %collective-permute-start.15 = (f32[96,128]{1,0:T(8,128)S(1)}, f32[96,128]{1,0:T(8,128)S(1)}, u32[]{:S(2)}, u32[]{:S(2)}) collective-permute-start(f32[96,128]{1,0:T(8,128)S(1)} %get-tuple-element.63), channel_id=1, source_target_pairs={{8,0},{16,8},{24,16},{0,24},{9,1},{17,9},{25,17},{1,25},{10,2},{18... | collective-permute-start | bytes 147464 | tf_op jit(solution)/shard_map/ppermute | solution.py:373
  58.8 6.0 %collective-permute-start.14 = (f32[96,128]{1,0:T(8,128)S(1)}, f32[96,128]{1,0:T(8,128)S(1)}, u32[]{:S(2)}, u32[]{:S(2)}) collective-permute-start(f32[96,128]{1,0:T(8,128)S(1)} %get-tuple-element.64), channel_id=1, source_target_pairs={{0,8},{8,16},{16,24},{24,0},{1,9},{9,17},{17,25},{25,1},{2,10},{10... | collective-permute-start | bytes 147464 | tf_op jit(solution)/shard_map/ppermute | solution.py:372
  58.8 5.9 %collective-permute-start.12 = (f32[2,16,128]{2,1,0:T(8,128)S(1)}, f32[2,16,128]{2,1,0:T(8,128)S(1)}, u32[]{:S(2)}, u32[]{:S(2)}) collective-permute-start(f32[2,16,128]{2,1,0:T(8,128)S(1)} %get-tuple-element.52), channel_id=1, source_target_pairs={{0,1},{1,2},{2,3},{3,4},{4,5},{5,6},{6,7},{7,0},{8,9},{9,10},{10,1... | collective-permute-start | bytes 49160 | tf_op jit(solution)/shard_map/ppermute | solution.py:368
  58.8 5.9 %collective-permute-start.13 = (f32[2,16,128]{2,1,0:T(8,128)S(1)}, f32[2,16,128]{2,1,0:T(8,128)S(1)}, u32[]{:S(2)}, u32[]{:S(2)}) collective-permute-start(f32[2,16,128]{2,1,0:T(8,128)S(1)} %get-tuple-element.53), channel_id=1, source_target_pairs={{1,0},{2,1},{3,2},{4,3},{5,4},{6,5},{7,6},{0,7},{9,8},{10,9},{11,1... | collective-permute-start | bytes 49160 | tf_op jit(solution)/shard_map/ppermute | solution.py:369

commit v2 on v1

--- a/solution.py
+++ b/solution.py
@@ -279,25 +279,29 @@
         parts, fill_planes = ("edge",), (0, planes + 1)
     else:
         start, parts, fill_planes = None, ("own", "edge"), range(planes + 2)
-        own, low, high, down, up, mixed = take(6)
+        own, down, up, mixed = take(4)
         now = take(1) + refs[-4:] if last else take(5)
         if last:
             del refs[-4:]
         scale = step_length * inverse_peak(mixed[:, mixed.shape[1] - 1, :])
-        for i, by in enumerate((own, low, high)):
-            now[i][...] = places[i][...] + scale.reshape((1,) * len(by.shape)) * by[...]
+        now[0][...] = places[0][...] + scale.reshape((1, 1, 1, 1)) * own[...]
+        pad = mixed.shape[1] // planes
+        for i, side in ((1, 5), (2, 4)):
+            for plane in range(planes):
+                by = mixed[ids[side], pl.ds(plane * pad, pad)]
+                now[i][plane] = places[i][plane] + scale * by
         for i, by, corners in ((3, down, (3, 2)), (4, up, (1, 0))):
-            base, pad = by.shape[0], mixed.shape[1]
+            base = by.shape[0]
             now[i][pl.ds(0, base)] = places[i][pl.ds(0, base)] + scale * by[...]
             for side, corner in enumerate(corners):
                 at = pl.ds(base + side * pad, pad)
-                now[i][at] = places[i][at] + scale * mixed[ids[corner]]
+                now[i][at] = places[i][at] + scale * mixed[ids[corner], pl.ds(0, pad)]
         places = now
     field = Field(places, planes, 3 * slots, rows)
     if last:
         force_ref, peak_ref, near = refs
     else:
-        force_ref, force_low, force_high, mix_ref, near = refs
+        force_ref, mix_ref, near = refs
     fill_near(field, near, fill_planes, 3 * slots, slots)
     totals = descent_sums(slots, planes, parts, start, barriers, field.own, near)
     peak = None
@@ -305,8 +309,6 @@
         forces = [total * weight_ref[plane, c % slots] for c, total in enumerate(totals[plane])]
         for c in range(3 * slots):
             force_ref[plane, c] = forces[c]
-            if not last:
-                put_rows(force_low, force_high, plane, c, forces[c])
         for s in range(slots):
             size = sum(forces[c * slots + s] * forces[c * slots + s] for c in range(3))
             peak = size if peak is None else jnp.maximum(peak, size)
@@ -320,10 +322,14 @@
         return carry
 
     lax.fori_loop(0, mix_ref.shape[0], fill, 0)
-    for corner in range(4):
-        plane = planes - 1 if corner < 2 else 0
-        rows_ref = force_high if corner % 2 == 0 else force_low
-        mix_ref[ids[corner], pl.ds(0, 3 * slots)] = rows_ref[plane, pl.ds(0, 3 * slots)]
+    pad = mix_ref.shape[1] // planes
+    for side in range(6):
+        step_y = 1 if side % 2 == 0 else -1
+        sent = range(planes) if side >= 4 else (planes - 1 if side < 2 else 0,)
+        for at, plane in enumerate(sent):
+            for c in range(3 * slots):
+                row = rows - 1 if step_y == 1 else 0
+                mix_ref[ids[side], pl.ds(at * pad + c, 1)] = force_ref[plane, c, pl.ds(row, 1)]
 
 
 def finish_kernel(place_ref, force_ref, peaks_ref, pos_ref, unit_ref):
@@ -362,25 +368,22 @@
     return down, up
 
 
-def near_halo(own, first_rows, last_rows):
+def near_planes(own):
     planes, channels, rows, lanes = own.shape
-    forward, backward = ring("sub")
-    low = lax.ppermute(last_rows, "sub", forward)
-    high = lax.ppermute(first_rows, "sub", backward)
     forward, backward = ring("slab")
     flat = (channels * rows, lanes)
     down = lax.ppermute(own[planes - 1].reshape(flat), "slab", forward)
     up = lax.ppermute(own[0].reshape(flat), "slab", backward)
-    return (own, low, high, down, up)
-
-
-def corner_devices():
+    return down, up
+
+
+def side_devices():
     slabs, subs = lax.axis_size("slab"), lax.axis_size("sub")
     x, y = lax.axis_index("slab"), lax.axis_index("sub")
     return jnp.stack(
         [
             ((x + i + slabs) % slabs) * subs + (y + j + subs) % subs
-            for i in (1, -1)
+            for i in (1, -1, 0)
             for j in (1, -1)
         ]
     ).astype(jnp.int32)
@@ -419,7 +422,7 @@
         for part, count in counts.items()
     }
     share = {part: flops * count // (27 * planes) for part, count in counts.items()}
-    ids = corner_devices()
+    ids = side_devices()
     flat = offsets.reshape(3 * slots, planes, *tiles)
     labels = chain_label.astype(jnp.float32)
     wide = jnp.concatenate([flat, labels], axis=0)
@@ -454,7 +457,7 @@
         def kernel(*refs, moving=bool(moves), final=final):
             descent_kernel(slots, planes, rows, moving, final, *refs)
 
-        outs = [field, (devices, lanes)] if final else [field, edge, edge, (devices, padded, lanes)]
+        outs = [field, (devices, lanes)] if final else [field, (devices, planes * padded, lanes)]
         moved = [x.shape for x in places] if moves else []
         scratch = [near]
         if final:
@@ -467,7 +470,7 @@
             break
         if moves:
             places, results = results[:5], results[5:]
-        moves = (*near_halo(*results[:3]), peaks)
+        moves = (results[0], *near_planes(results[0]), peaks)
     positions, unit_force = call(finish_kernel, [offsets.shape, offsets.shape])(
         place, force, peaks
     )

time: 82.9 us -> 92.5 us (1.12)
  waiting for transfers between devices: 10.1 us -> 29.7 us
  starting transfers between devices: 34.6 us -> 26.1 us
  blocking collectives: 11 us -> 9.19 us
    all_to_all x2, waiting for transfers between devices: 2.61 us -> 14 us  [shards(): peaks = lax.all_to_all(results[-1], ('slab', 'sub'), 0, 0, tiled=True)]
    ppermute x8 -> x4, waiting for transfers between devices: 4.81 us -> 13.1 us  [the longest x2 9.98 us: near_planes(): up = lax.ppermute(own[0].reshape(flat), 'slab', backward)]
    ppermute x8 -> x4, starting transfers between devices: 12.5 us -> 5.35 us  [the longest x2 5.34 us: near_planes(): up = lax.ppermute(own[0].reshape(flat), 'slab', backward)]
    all_to_all x1, blocking collectives: 11 us -> 9.19 us  [shards(): peaks = lax.all_to_all(results[-1], ('slab', 'sub'), 0, 0, tiled=True)]
    all_to_all x2, starting transfers between devices: 7.94 us -> 6.59 us  [shards(): peaks = lax.all_to_all(results[-1], ('slab', 'sub'), 0, 0, tiled=True)]
  transfers between devices with their start and end apart: 18 -> 14, of which waited for: 7 -> 9; matrix products, arithmetic and copies ran while one was open for 2% -> 2% of each run, Pallas kernels for 7% -> 7%
where the time goes in v2:
time: 92.5 us; the launch traced here: 92.1 us
  waiting for transfers between devices  29.7 us (32%)
  starting transfers between devices  26.1 us (28%)
  Pallas kernels  22.8 us (25%)
  blocking collectives  9.19 us (10%)
  other arithmetic  3.35 us (4%)
    all_to_all x2, waiting for transfers between devices, shards(): peaks = lax.all_to_all(results[-1], ('slab', 'sub'), 0, 0, tiled=True)  14 us
    pallas_call x3, Pallas kernels, shards(): call(kernel, moved + outs, scratch, flops, 1, len(operands))(*operands)  13.5 us
    ppermute x2, waiting for transfers between devices, near_planes(): up = lax.ppermute(own[0].reshape(flat), 'slab', backward)  9.98 us
    all_to_all x1, blocking collectives, shards(): peaks = lax.all_to_all(results[-1], ('slab', 'sub'), 0, 0, tiled=True)  9.19 us
    ppermute x2, starting transfers between devices, row_halo(): lax.ppermute(first_rows, 'sub', backward)  7.63 us
    all_to_all x2, starting transfers between devices, shards(): peaks = lax.all_to_all(results[-1], ('slab', 'sub'), 0, 0, tiled=True)  6.59 us
    ppermute x2, starting transfers between devices, near_planes(): up = lax.ppermute(own[0].reshape(flat), 'slab', backward)  5.34 us
    ppermute x2, starting transfers between devices, plane_halo(): down = lax.ppermute(packed(planes - 1), 'slab', forward)  3.68 us
  transfers between devices with their start and end apart: 14, of which 9 were waited for; matrix products, arithmetic and copies ran while one was open for 2% of the time, Pallas kernels for 7%

profile of v2, /device:TPU:0, one launch (start us, length us, event | category | flops | bytes accessed | tf_op | source)
XLA Modules:
  0.0 92.1 jit_solution(10797624601316554705)
XLA Ops:
  0.6 0.0 copy-start
  0.6 0.8 convert_element_type.15
  1.4 0.9 pad_maximum_fusion.1.wide_ref
  2.4 0.5 collective-permute-start
  2.9 4.1 %collective-permute-start.1 = (f32[2,16,128]{2,1,0:T(8,128)S(1)}, f32[2,16,128]{2,1,0:T(8,128)S(1)}, u32[]{:S(2)}, u32[]{:S(2)}) collective-permute-start(f32[2,16,128]{2,1,0:T(8,128)S(1)} %get-tuple-element.30), channel_id=1, source_target_pairs={{1,0},{2,1},{3,2},{4,3},{5,4},{6,5},{7,6},{0,7},{9,8},{10,9},{11,1... | collective-permute-start | bytes 49160 | tf_op jit(solution)/shard_map/ppermute | solution.py:354
  7.0 0.8 convert_element_type.14
  7.8 0.8 convert_element_type.12
  8.6 0.0 collective-permute-done.low
  8.7 0.0 collective-permute-done.1.high
  8.7 2.0 %collective-permute-start.2 = (f32[160,128]{1,0:T(8,128)S(1)}, f32[160,128]{1,0:T(8,128)S(1)}, u32[]{:S(2)}, u32[]{:S(2)}) collective-permute-start(f32[160,128]{1,0:T(8,128)S(1)} %pad_maximum_fusion.2), channel_id=1, source_target_pairs={{0,8},{8,16},{16,24},{24,0},{1,9},{9,17},{17,25},{25,1},{2,10},{10... | collective-permute-start | bytes 245768 | tf_op jit(solution)/shard_map/ppermute | solution.py:366
  10.7 1.0 %collective-permute-start.3 = (f32[160,128]{1,0:T(8,128)S(1)}, f32[160,128]{1,0:T(8,128)S(1)}, u32[]{:S(2)}, u32[]{:S(2)}) collective-permute-start(f32[160,128]{1,0:T(8,128)S(1)} %pad_maximum_fusion.3), channel_id=1, source_target_pairs={{8,0},{16,8},{24,16},{0,24},{9,1},{17,9},{25,17},{1,25},{10,2},{18... | collective-permute-start | bytes 245768 | tf_op jit(solution)/shard_map/ppermute | solution.py:367
  11.7 0.0 copy-done
  11.7 3.4 %shard_map.77 = (f32[2,12,8,128]{3,2,1,0:T(8,128)S(1)}, bf16[36,8,16,128]{3,2,1,0:T(8,128)(2,1)S(1)}) custom-call(f32[24,2,8,128]{3,2,1,0:T(8,128)S(1)} %pad_maximum_fusion.extra_ref, f32[2,16,8,128]{3,2,1,0:T(8,128)S(1)} %get-tuple-element.28.own, f32[2,16,128]{2,1,0:T(8,128)S(1)} %collective-permute-done.low, f32[2,16,128]{2,1,0:T(8,128)S(1)} %collective-permute-done.1.high), custom_call_target="tpu_custom_call" | custom-call | flops 17694720 | bytes 4194304 | tf_op jit(solution)/shard_map/pallas_call | solution.py:440
  15.2 0.0 collective-permute-done.2.down
  15.2 0.9 %collective-permute-done.3.up = f32[160,128]{1,0:T(8,128)S(1)} collective-permute-done((f32[160,128]{1,0:T(8,128)S(1)}, f32[160,128]{1,0:T(8,128)S(1)}, u32[]{:S(2)}, u32[]{:S(2)}) %collective-permute-start.3) | collective-permute-done | bytes 81952 | tf_op jit(solution)/shard_map/ppermute | solution.py:367
  16.1 2.4 %shard_map.78 = (f32[3,4,2,8,128]{4,3,2,1,0:T(8,128)}, f32[2,12,8,128]{3,2,1,0:T(8,128)S(1)}, f32[2,16,128]{2,1,0:T(8,128)S(1)}, f32[2,16,128]{2,1,0:T(8,128)S(1...) custom-call(f32[24,2,8,128]{3,2,1,0:T(8,128)S(1)} %pad_maximum_fusion.extra_ref, ...), custom_call_target="tpu_custom_call" | custom-call | flops 8847360 | bytes 4194304 | tf_op jit(solution)/shard_map/pallas_call | solution.py:444
  18.5 0.0 collective-permute-start.4
  18.5 3.5 %collective-permute-start.5 = (f32[2,16,128]{2,1,0:T(8,128)S(1)}, f32[2,16,128]{2,1,0:T(8,128)S(1)}, u32[]{:S(2)}, u32[]{:S(2)}) collective-permute-start(f32[2,16,128]{2,1,0:T(8,128)S(1)} %get-tuple-element.37), channel_id=1, source_target_pairs={{1,0},{2,1},{3,2},{4,3},{5,4},{6,5},{7,6},{0,7},{9,8},{10,9},{11,1... | collective-permute-start | bytes 49160 | tf_op jit(solution)/shard_map/ppermute | solution.py:354
  22.1 1.5 %collective-permute-done.4.low.refs_5_ = f32[2,16,128]{2,1,0:T(8,128)S(1)} collective-permute-done((f32[2,16,128]{2,1,0:T(8,128)S(1)}, f32[2,16,128]{2,1,0:T(8,128)S(1)}, u32[]{:S(2)}, u32[]{:S(2)}) %collective-permute-start.4) | collective-permute-done | bytes 16416 | tf_op jit(solution)/shard_map/ppermute | solution.py:354
  23.6 0.0 collective-permute-done.5.high.refs_6_
  23.6 1.7 %collective-permute-start.6 = (f32[128,128]{1,0:T(8,128)S(1)}, f32[128,128]{1,0:T(8,128)S(1)}, u32[]{:S(2)}, u32[]{:S(2)}) collective-permute-start(f32[128,128]{1,0:T(8,128)S(1)} %pad_maximum_fusion.4), channel_id=1, source_target_pairs={{0,8},{8,16},{16,24},{24,0},{1,9},{9,17},{17,25},{25,1},{2,10},{10... | collective-permute-start | bytes 196616 | tf_op jit(solution)/shard_map/ppermute | solution.py:366
  25.3 1.3 %collective-permute-start.7 = (f32[128,128]{1,0:T(8,128)S(1)}, f32[128,128]{1,0:T(8,128)S(1)}, u32[]{:S(2)}, u32[]{:S(2)}) collective-permute-start(f32[128,128]{1,0:T(8,128)S(1)} %pad_maximum_fusion.5), channel_id=1, source_target_pairs={{8,0},{16,8},{24,16},{0,24},{9,1},{17,9},{25,17},{1,25},{10,2},{18... | collective-permute-start | bytes 196616 | tf_op jit(solution)/shard_map/ppermute | solution.py:367
  26.6 0.1 stack.27.refs_0_
  26.7 2.7 %shard_map.79.refs_9_ = f32[2,12,8,128]{3,2,1,0:T(8,128)S(1)} custom-call(bf16[36,8,16,128]{3,2,1,0:T(8,128)(2,1)S(1)} %get-tuple-element.31.barrier_ref.refs_1_, f32[2,12,8,128]{3,2,1,0:T(8,128)S(1)} %get-tuple-element.35.own.refs_4_, f32[2,16,128]{2,1,0:T(8,128)S(1)} %collective-permute-done.4.low.refs_5_, ...), custom_call_target="tpu_custom_call" | custom-call | flops 17694720 | bytes 4194304 | tf_op jit(solution)/shard_map/pallas_call | solution.py:451
  29.4 0.0 collective-permute-done.6.refs_7_
  29.4 0.2 collective-permute-done.7.refs_8_
  29.6 3.0 %shard_map.80 = (f32[2,12,8,128]{3,2,1,0:T(8,128)S(1)}, f32[32,32,128]{2,1,0:T(8,128)}) custom-call(s32[6]{0:T(128)S(1)} %stack.27.refs_0_, bf16[36,8,16,128]{3,2,1,0:T(8,128)(2,1)S(1)} %get-tuple-element.31.barrier_ref.refs_1_, bf16[18,8,16,128]{3,2,1,0:T(8,128)(2,1)S(1)} %get-tuple-element.33.refs_2_, f32[2,4,8,128]{3,2,1,0:T(8,128)S(1)} %get-tuple-element.34.refs_3_, ...), custom_call_target="tpu_custom_call" | custom-call | flops 26542080 | bytes 4194304 | tf_op jit(solution)/shard_map/pallas_call | solution.py:466
  32.5 4.0 %all-to-all-start = ((f32[32,32,128]{2,1,0:T(8,128)}), f32[32,32,128]{2,1,0:T(8,128)S(1)}, u32[]{:S(2)}, u32[]{:S(2)}) async-start(f32[32,32,128]{2,1,0:T(8,128)} %get-tuple-element.39), calls=%async_computation | async-start | bytes 1048576 | tf_op jit(solution)/shard_map/all_to_all | solution.py:467
  36.6 2.7 %collective-permute-start.9 = (f32[96,128]{1,0:T(8,128)S(1)}, f32[96,128]{1,0:T(8,128)S(1)}, u32[]{:S(2)}, u32[]{:S(2)}) collective-permute-start(f32[96,128]{1,0:T(8,128)S(1)} %get-tuple-element.57), channel_id=1, source_target_pairs={{8,0},{16,8},{24,16},{0,24},{9,1},{17,9},{25,17},{1,25},{10,2},{18... | collective-permute-start | bytes 147464 | tf_op jit(solution)/shard_map/ppermute | solution.py:376
  39.3 0.0 collective-permute-start.8
  39.3 5.0 %collective-permute-done.9.refs_11_ = f32[96,128]{1,0:T(8,128)S(1)} collective-permute-done((f32[96,128]{1,0:T(8,128)S(1)}, f32[96,128]{1,0:T(8,128)S(1)}, u32[]{:S(2)}, u32[]{:S(2)}) %collective-permute-start.9) | collective-permute-done | bytes 49184 | tf_op jit(solution)/shard_map/ppermute | solution.py:376
  44.3 1.6 %collective-permute-done.8.refs_10_ = f32[96,128]{1,0:T(8,128)S(1)} collective-permute-done((f32[96,128]{1,0:T(8,128)S(1)}, f32[96,128]{1,0:T(8,128)S(1)}, u32[]{:S(2)}, u32[]{:S(2)}) %collective-permute-start.8) | collective-permute-done | bytes 49184 | tf_op jit(solution)/shard_map/ppermute | solution.py:375
  45.9 6.9 %all-to-all-done.refs_12_ = f32[32,32,128]{2,1,0:T(8,128)S(1)} async-done(((f32[32,32,128]{2,1,0:T(8,128)}), f32[32,32,128]{2,1,0:T(8,128)S(1)}, u32[]{:S(2)}, u32[]{:S(2)}) %all-to-all-start) | async-done | bytes 524320 | tf_op jit(solution)/shard_map/all_to_all | solution.py:467
  52.8 5.8 %shard_map.81 = (f32[2,12,8,128]{3,2,1,0:T(8,128)S(1)}, f32[2,16,128]{2,1,0:T(8,128)S(1)}, f32[2,16,128]{2,1,0:T(8,128)S(1)}, f32[128,128]{1,0:T(8,128)S(1)}, f3...) custom-call(s32[6]{0:T(128)S(1)} %stack.27.refs_0_, ...), custom_call_target="tpu_custom_call" | custom-call | flops 26542080 | bytes 4194304 | tf_op jit(solution)/shard_map/pallas_call | solution.py:466
  58.5 2.6 %all-to-all-start.1 = ((f32[32,32,128]{2,1,0:T(8,128)}), f32[32,32,128]{2,1,0:T(8,128)S(1)}, u32[]{:S(2)}, u32[]{:S(2)}) async-start(f32[32,32,128]{2,1,0:T(8,128)} %get-tuple-element.46), calls=%async_computation.1 | async-start | bytes 1048576 | tf_op jit(solution)/shard_map/all_to_all | solution.py:467
  61.2 2.6 %collective-permute-start.11 = (f32[96,128]{1,0:T(8,128)S(1)}, f32[96,128]{1,0:T(8,128)S(1)}, u32[]{:S(2)}, u32[]{:S(2)}) collective-permute-start(f32[96,128]{1,0:T(8,128)S(1)} %get-tuple-element.55), channel_id=1, source_target_pairs={{8,0},{16,8},{24,16},{0,24},{9,1},{17,9},{25,17},{1,25},{10,2},{18... | collective-permute-start | bytes 147464 | tf_op jit(solution)/shard_map/ppermute | solution.py:376
  63.8 0.0 collective-permute-start.10
  63.8 5.0 %collective-permute-done.11.refs_11_ = f32[96,128]{1,0:T(8,128)S(1)} collective-permute-done((f32[96,128]{1,0:T(8,128)S(1)}, f32[96,128]{1,0:T(8,128)S(1)}, u32[]{:S(2)}, u32[]{:S(2)}) %collective-permute-start.11) | collective-permute-done | bytes 49184 | tf_op jit(solution)/shard_map/ppermute | solution.py:376
  68.8 1.6 %collective-permute-done.10.refs_10_ = f32[96,128]{1,0:T(8,128)S(1)} collective-permute-done((f32[96,128]{1,0:T(8,128)S(1)}, f32[96,128]{1,0:T(8,128)S(1)}, u32[]{:S(2)}, u32[]{:S(2)}) %collective-permute-start.10) | collective-permute-done | bytes 49184 | tf_op jit(solution)/shard_map/ppermute | solution.py:375
  70.3 7.1 %all-to-all-done.1.refs_12_ = f32[32,32,128]{2,1,0:T(8,128)S(1)} async-done(((f32[32,32,128]{2,1,0:T(8,128)}), f32[32,32,128]{2,1,0:T(8,128)S(1)}, u32[]{:S(2)}, u32[]{:S(2)}) %all-to-all-start.1) | async-done | bytes 524320 | tf_op jit(solution)/shard_map/all_to_all | solution.py:467
  77.4 4.7 %shard_map.82 = (f32[2,12,8,128]{3,2,1,0:T(8,128)S(1)}, f32[2,12,8,128]{3,2,1,0:T(8,128)S(1)}, f32[32,128]{1,0:T(8,128)S(1)}) custom-call(s32[6]{0:T(128)S(1)} %stack.27.refs_0_, bf16[36,8,16,128]{3,2,1,0:T(8,128)(2,1)S(1)} %get-tuple-element.31.barrier_ref.refs_1_, bf16[18,8,16,128]{3,2,1,0:T(8,128)(2,1)S(1)} %get-tuple-element.33.refs_2_, ...), custom_call_target="tpu_custom_call" | custom-call | flops 26542080 | bytes 4194304 | tf_op jit(solution)/shard_map/pallas_call | solution.py:466
  82.1 9.2 %all_to_all.21 = f32[32,1,128]{2,1,0:T(1,128)S(1)} all-to-all(f32[32,1,128]{2,1,0:T(1,128)S(1)} %bitcast.46), channel_id=1, replica_groups=mesh['slab'=4,'sub'=8] {'slab','sub'}, dimensions={0} | all-to-all | bytes 32768 | tf_op jit(solution)/shard_map/all_to_all | solution.py:467
  91.3 0.8 shard_map.83
  (14 shorter events, 0.1 us)
Async XLA Ops:
  0.6 11.1 %copy-start = (f32[3,4,2,8,128]{4,3,2,1,0:T(8,128)S(1)}, f32[3,4,2,8,128]{4,3,2,1,0:T(8,128)}, u32[]{:S(2)}) copy-start(f32[3,4,2,8,128]{4,3,2,1,0:T(8,128)} %param.6) | copy-start | bytes 294916
  2.4 6.3 %collective-permute-start = (f32[2,16,128]{2,1,0:T(8,128)S(1)}, f32[2,16,128]{2,1,0:T(8,128)S(1)}, u32[]{:S(2)}, u32[]{:S(2)}) collective-permute-start(f32[2,16,128]{2,1,0:T(8,128)S(1)} %get-tuple-element.29), channel_id=1, source_target_pairs={{0,1},{1,2},{2,3},{3,4},{4,5},{5,6},{6,7},{7,0},{8,9},{9,10},{10,1... | collective-permute-start | bytes 49160 | tf_op jit(solution)/shard_map/ppermute | solution.py:354
  2.9 5.7 %collective-permute-start.1 = (f32[2,16,128]{2,1,0:T(8,128)S(1)}, f32[2,16,128]{2,1,0:T(8,128)S(1)}, u32[]{:S(2)}, u32[]{:S(2)}) collective-permute-start(f32[2,16,128]{2,1,0:T(8,128)S(1)} %get-tuple-element.30), channel_id=1, source_target_pairs={{1,0},{2,1},{3,2},{4,3},{5,4},{6,5},{7,6},{0,7},{9,8},{10,9},{11,1... | collective-permute-start | bytes 49160 | tf_op jit(solution)/shard_map/ppermute | solution.py:354
  8.7 6.5 %collective-permute-start.2 = (f32[160,128]{1,0:T(8,128)S(1)}, f32[160,128]{1,0:T(8,128)S(1)}, u32[]{:S(2)}, u32[]{:S(2)}) collective-permute-start(f32[160,128]{1,0:T(8,128)S(1)} %pad_maximum_fusion.2), channel_id=1, source_target_pairs={{0,8},{8,16},{16,24},{24,0},{1,9},{9,17},{17,25},{25,1},{2,10},{10... | collective-permute-start | bytes 245768 | tf_op jit(solution)/shard_map/ppermute | solution.py:366
  10.7 5.4 %collective-permute-start.3 = (f32[160,128]{1,0:T(8,128)S(1)}, f32[160,128]{1,0:T(8,128)S(1)}, u32[]{:S(2)}, u32[]{:S(2)}) collective-permute-start(f32[160,128]{1,0:T(8,128)S(1)} %pad_maximum_fusion.3), channel_id=1, source_target_pairs={{8,0},{16,8},{24,16},{0,24},{9,1},{17,9},{25,17},{1,25},{10,2},{18... | collective-permute-start | bytes 245768 | tf_op jit(solution)/shard_map/ppermute | solution.py:367
  18.5 5.1 %collective-permute-start.4 = (f32[2,16,128]{2,1,0:T(8,128)S(1)}, f32[2,16,128]{2,1,0:T(8,128)S(1)}, u32[]{:S(2)}, u32[]{:S(2)}) collective-permute-start(f32[2,16,128]{2,1,0:T(8,128)S(1)} %get-tuple-element.36), channel_id=1, source_target_pairs={{0,1},{1,2},{2,3},{3,4},{4,5},{5,6},{6,7},{7,0},{8,9},{9,10},{10,1... | collective-permute-start | bytes 49160 | tf_op jit(solution)/shard_map/ppermute | solution.py:354
  18.5 5.1 %collective-permute-start.5 = (f32[2,16,128]{2,1,0:T(8,128)S(1)}, f32[2,16,128]{2,1,0:T(8,128)S(1)}, u32[]{:S(2)}, u32[]{:S(2)}) collective-permute-start(f32[2,16,128]{2,1,0:T(8,128)S(1)} %get-tuple-element.37), channel_id=1, source_target_pairs={{1,0},{2,1},{3,2},{4,3},{5,4},{6,5},{7,6},{0,7},{9,8},{10,9},{11,1... | collective-permute-start | bytes 49160 | tf_op jit(solution)/shard_map/ppermute | solution.py:354
  23.6 5.8 %collective-permute-start.6 = (f32[128,128]{1,0:T(8,128)S(1)}, f32[128,128]{1,0:T(8,128)S(1)}, u32[]{:S(2)}, u32[]{:S(2)}) collective-permute-start(f32[128,128]{1,0:T(8,128)S(1)} %pad_maximum_fusion.4), channel_id=1, source_target_pairs={{0,8},{8,16},{16,24},{24,0},{1,9},{9,17},{17,25},{25,1},{2,10},{10... | collective-permute-start | bytes 196616 | tf_op jit(solution)/shard_map/ppermute | solution.py:366
  25.3 4.3 %collective-permute-start.7 = (f32[128,128]{1,0:T(8,128)S(1)}, f32[128,128]{1,0:T(8,128)S(1)}, u32[]{:S(2)}, u32[]{:S(2)}) collective-permute-start(f32[128,128]{1,0:T(8,128)S(1)} %pad_maximum_fusion.5), channel_id=1, source_target_pairs={{8,0},{16,8},{24,16},{0,24},{9,1},{17,9},{25,17},{1,25},{10,2},{18... | collective-permute-start | bytes 196616 | tf_op jit(solution)/shard_map/ppermute | solution.py:367
  32.5 20.2 %all-to-all-start = ((f32[32,32,128]{2,1,0:T(8,128)}), f32[32,32,128]{2,1,0:T(8,128)S(1)}, u32[]{:S(2)}, u32[]{:S(2)}) async-start(f32[32,32,128]{2,1,0:T(8,128)} %get-tuple-element.39), calls=%async_computation | async-start | bytes 1048576 | tf_op jit(solution)/shard_map/all_to_all | solution.py:467
  36.6 7.7 %collective-permute-start.9 = (f32[96,128]{1,0:T(8,128)S(1)}, f32[96,128]{1,0:T(8,128)S(1)}, u32[]{:S(2)}, u32[]{:S(2)}) collective-permute-start(f32[96,128]{1,0:T(8,128)S(1)} %get-tuple-element.57), channel_id=1, source_target_pairs={{8,0},{16,8},{24,16},{0,24},{9,1},{17,9},{25,17},{1,25},{10,2},{18... | collective-permute-start | bytes 147464 | tf_op jit(solution)/shard_map/ppermute | solution.py:376
  39.3 6.6 %collective-permute-start.8 = (f32[96,128]{1,0:T(8,128)S(1)}, f32[96,128]{1,0:T(8,128)S(1)}, u32[]{:S(2)}, u32[]{:S(2)}) collective-permute-start(f32[96,128]{1,0:T(8,128)S(1)} %get-tuple-element.58), channel_id=1, source_target_pairs={{0,8},{8,16},{16,24},{24,0},{1,9},{9,17},{17,25},{25,1},{2,10},{10... | collective-permute-start | bytes 147464 | tf_op jit(solution)/shard_map/ppermute | solution.py:375
  58.5 18.8 %all-to-all-start.1 = ((f32[32,32,128]{2,1,0:T(8,128)}), f32[32,32,128]{2,1,0:T(8,128)S(1)}, u32[]{:S(2)}, u32[]{:S(2)}) async-start(f32[32,32,128]{2,1,0:T(8,128)} %get-tuple-element.46), calls=%async_computation.1 | async-start | bytes 1048576 | tf_op jit(solution)/shard_map/all_to_all | solution.py:467
  61.2 7.6 %collective-permute-start.11 = (f32[96,128]{1,0:T(8,128)S(1)}, f32[96,128]{1,0:T(8,128)S(1)}, u32[]{:S(2)}, u32[]{:S(2)}) collective-permute-start(f32[96,128]{1,0:T(8,128)S(1)} %get-tuple-element.55), channel_id=1, source_target_pairs={{8,0},{16,8},{24,16},{0,24},{9,1},{17,9},{25,17},{1,25},{10,2},{18... | collective-permute-start | bytes 147464 | tf_op jit(solution)/shard_map/ppermute | solution.py:376
  63.8 6.5 %collective-permute-start.10 = (f32[96,128]{1,0:T(8,128)S(1)}, f32[96,128]{1,0:T(8,128)S(1)}, u32[]{:S(2)}, u32[]{:S(2)}) collective-permute-start(f32[96,128]{1,0:T(8,128)S(1)} %get-tuple-element.56), channel_id=1, source_target_pairs={{0,8},{8,16},{16,24},{24,0},{1,9},{9,17},{17,25},{25,1},{2,10},{10... | collective-permute-start | bytes 147464 | tf_op jit(solution)/shard_map/ppermute | solution.py:375
